TPU v7x, 256 devices: a whole 4x4x8 slice. The times are simulated.
256 devices in a mesh: dp: 8 (over y, core), expert: 8 (over z), ffn: 4 (over x).
Axes of the slice: x: 4, y: 4, z: 8, core: 2. Of those that a mesh axis runs over, the one named last changes fastest.
Arguments:
- tokens: bfloat16 [512, 6144], P(('dp', 'expert'), 'ffn'), may hold values from -6 to 6
- out_grad: bfloat16 [512, 6144], P(('dp', 'expert'), 'ffn'), may hold values from -6 to 6
- expert_ids: int32 [512, 2], P(('dp', 'expert')), may hold values from 0 to 7, all different within a row; in each aligned block of 8 rows (0 to 7, 8 to 15, ...) at most 3 rows name the same one
- tenant_ids: int32 [512], P(('dp', 'expert')), may hold values from 0 to 7
- router_logits: float32 [512, 2], P(('dp', 'expert')), may hold values from -8 to 8
- gate_projection_weight: bfloat16 [8, 6144, 8192], P('expert', None, ('dp', 'ffn')), may hold values from -0.078125 to 0.078125
- up_projection_weight: bfloat16 [8, 6144, 8192], P('expert', None, ('dp', 'ffn')), may hold values from -0.078125 to 0.078125
- down_projection_weight: bfloat16 [8, 8192, 6144], P('expert', ('dp', 'ffn')), may hold values from -0.0625 to 0.0625
- input_down_maps: bfloat16 [8, 6144, 256], P('expert', 'ffn'), may hold values from -0.078125 to 0.078125
- input_up_maps: bfloat16 [8, 2, 128, 8192], P('expert', None, None, ('dp', 'ffn')), may hold values from -1.5 to 1.5
- output_down_map: bfloat16 [8, 8192, 128], P('expert', ('dp', 'ffn')), may hold values from -0.0625 to 0.0625
- output_up_map: bfloat16 [8, 128, 6144], P('expert', None, 'ffn'), may hold values from -1.5 to 1.5
Outputs:
- mixed: bfloat16 [512, 6144], P(('dp', 'expert'), 'ffn')
- input_grad: bfloat16 [512, 6144], P(('dp', 'expert'), 'ffn')
- input_down_gradient: float32 [8, 6144, 256], P('expert', 'ffn')
- input_up_gradient: float32 [8, 2, 128, 8192], P('expert', None, None, ('dp', 'ffn'))
- output_down_gradient: float32 [8, 8192, 128], P('expert', ('dp', 'ffn'))
- output_up_gradient: float32 [8, 128, 6144], P('expert', None, 'ffn')
Inputs may be any that keep to these rules, and one draw needn't show every extreme that they name: `expert_ids`: each row names 2 different experts. Among the rows of one device's block of 8 tokens no expert is named more than 3 times; in some blocks one expert is named exactly 3 times.
All inputs are finite; a program needn't handle non-finite values.
Results may differ from a plain program's by a relative error of at most 0.0073.
Values may be sent and summed in bfloat16 or wider, within the bound.
No kernel may reach another device: no remote copies, remote signals or barrier semaphores. Data moves between devices by JAX's collectives and lax.ppermute only.
A program may use at most 256 MiB of HBM per device.

v0:
```python
import functools

import jax
import jax.numpy as jnp
from jax import lax
from jax.experimental import pallas as pl
from jax.experimental.pallas import tpu as pltpu
from jax.sharding import PartitionSpec as P


RANK = 16
SCALE = 0.5
SLOTS = 3
GROUP = 8
LANES = 128
BF = jnp.bfloat16
F32 = jnp.float32
I32 = jnp.int32


def dot(left, right, dims=((1,), (0,))):
    return lax.dot_general(left, right, (dims, ((), ())), preferred_element_type=F32)


def rows_of(shape):
    return lax.broadcasted_iota(I32, shape, 0)


def lanes_of(shape):
    return lax.broadcasted_iota(I32, shape, 1)


def onehot(condition):
    return jnp.where(condition, 1.0, 0.0).astype(BF)


def two_parts(value):
    high = value.astype(BF)
    return high, (value - high.astype(F32)).astype(BF)


def vmem():
    return pl.BlockSpec(memory_space=pltpu.VMEM)


def smem():
    return pl.BlockSpec(memory_space=pltpu.SMEM)


def anywhere():
    return pl.BlockSpec(memory_space=pl.ANY)


def place_of(where):
    return where[0], where[1], where[2]


def codes_of(ids):
    n_top, n_rows = ids.shape
    chosen = [ids[k, t] for t in range(n_rows) for k in range(n_top)]
    codes = []
    for i, expert in enumerate(chosen):
        position = jnp.int32(0)
        for earlier in chosen[:i]:
            position += jnp.where(earlier == expert, 1, 0).astype(I32)
        codes.append((i // n_top, i % n_top, expert, position))
    return codes


def gates(logits):
    n_rows = logits.shape[1]
    first = jax.nn.sigmoid(logits[0:1, :] - logits[1:2, :])
    diagonal = rows_of((n_rows, n_rows)) == lanes_of((n_rows, n_rows))
    first = jnp.sum(jnp.where(diagonal, first, 0.0), axis=1, keepdims=True)
    return first, 1.0 - first


def dispatch_kernel(ids, tenants, logits, tokens, grads, out):
    n_out = out.shape[0]
    n_rows = tokens.shape[0]
    codes = codes_of(ids)
    first, second = gates(logits[...])
    row = rows_of((n_out, LANES))
    lane = lanes_of((n_out, LANES))
    pick_token = jnp.zeros((n_out, LANES), F32)
    pick_grad = jnp.zeros((n_out, LANES), F32)
    tenant_row = jnp.zeros((n_out, LANES), F32)
    for t, k, expert, position in codes:
        base = expert * GROUP
        pick_token = jnp.where((row == base + position) & (lane == t), 1.0, pick_token)
        pick_grad = jnp.where(
            (row == base + SLOTS + position) & (lane == t + k * n_rows), 1.0, pick_grad
        )
        code = (tenants[t] + 1).astype(F32)
        tenant_row = jnp.where(
            (row == base + 2 * SLOTS) & (lane == position), code, tenant_row
        )
    g = grads[...].astype(F32)
    scaled = jnp.concatenate([(first * g).astype(BF), (second * g).astype(BF)], axis=0)
    value = dot(pick_token[:, :n_rows].astype(BF), tokens[...]) + dot(
        pick_grad[:, : 2 * n_rows].astype(BF), scaled
    )
    out[...] = value.astype(BF)
    out[:, :LANES] = (value[:, :LANES] + tenant_row).astype(BF)


def received_kernel(where, arrived, down_maps, up_map, keep, send):
    n_in, width = arrived.shape
    n = keep.shape[0]
    core = where[2]
    row = rows_of((n, n_in))
    column = lanes_of((n, n_in))
    start = (row // SLOTS) * GROUP
    offset = row % SLOTS
    data = arrived[...]
    tokens = dot(onehot(column == start + offset), data).astype(BF)
    grads = dot(onehot(column == start + SLOTS + offset), data).astype(BF)
    tenants = dot(onehot(column == start + 2 * SLOTS), data[:, :LANES])
    lane = lanes_of((n, LANES))
    tenant = jnp.sum(
        jnp.where(lane == rows_of((n, LANES)) % SLOTS, tenants, 0.0), axis=1, keepdims=True
    )
    mask = jnp.where((lane // RANK + 1).astype(F32) == tenant, 1.0, 0.0)
    product = dot(tokens, down_maps[0])
    back = dot(grads, up_map[0], ((1,), (1,)))
    source = rows_of((LANES, LANES)) % RANK
    target = lanes_of((LANES, LANES))

    def moved(value, offset):
        return dot(value, onehot(target - offset == source))

    gate_high, gate_low = two_parts(mask * product[:, :LANES])
    up_high, up_low = two_parts(mask * product[:, LANES:])
    back_high, back_low = two_parts(mask * back)
    token_extra = (
        moved(gate_high, 0)
        + moved(up_high, RANK)
        + moved(gate_low, 2 * RANK)
        + moved(up_low, 3 * RANK)
        + jnp.where(lane == 4 * RANK, tenant, 0.0)
    ).astype(BF)
    grad_extra = (moved(back_high, 0) + moved(back_low, RANK)).astype(BF)

    @pl.when(core == 0)
    def _():
        keep[:, :width] = tokens
        keep[:, width:] = token_extra
        send[:, :width] = grads
        send[:, width:] = grad_extra

    @pl.when(core != 0)
    def _():
        keep[:, :width] = grads
        keep[:, width:] = grad_extra
        send[:, :width] = tokens
        send[:, width:] = token_extra


def unit_kernel(where, mine, theirs, out):
    n = mine.shape[0]

    @pl.when(where[2] == 0)
    def _():
        out[:n] = mine[...]
        out[n:] = theirs[...]

    @pl.when(where[2] != 0)
    def _():
        out[:n] = theirs[...]
        out[n:] = mine[...]


def stack_kernel(first, second, *rest):
    out = rest[-1]
    out[0] = first[...]
    out[1] = second[...]


def maps_kernel(down_maps, up_map, down_maps_v, up_map_v, sem):
    copies = [
        pltpu.make_async_copy(down_maps, down_maps_v, sem),
        pltpu.make_async_copy(up_map, up_map_v, sem),
    ]
    for c in copies:
        c.start()
    for c in copies:
        c.wait()


def weights_kernel(where, gate_w, up_w, down_w, _, gate_v, up_v, down_v, sem):
    n, _, width = down_v.shape
    copy = pltpu.make_async_copy
    copies = []
    for s in range(n):
        span = pl.ds(pl.multiple_of(((where[0] - s + n) % n) * width, width), width)
        copies += [
            copy(gate_w.at[0, span, :], gate_v.at[pl.ds(s * width, width)], sem),
            copy(up_w.at[0, span, :], up_v.at[pl.ds(s * width, width)], sem),
            copy(down_w.at[0, :, span], down_v.at[s], sem),
        ]
    for c in copies:
        c.start()
    for c in copies:
        c.wait()


def turned_weights_kernel(gate_v, up_v, down_v, both_t, down_t):
    n, hidden, width = down_v.shape
    for s in range(n):
        span = slice(s * width, (s + 1) * width)
        both_t[s, :hidden] = gate_v[span].T
        both_t[s, hidden:] = up_v[span].T
        down_t[span] = down_v[s].T


def expert_kernel(where, *refs):
    n = 4
    halves = [refs[2 * k : 2 * k + 2] for k in range(2 * n)]
    own, far = halves[:n], halves[n:]
    gate_w, up_w, down_w, down_t, up_maps, out_down = refs[4 * n : 4 * n + 6]
    parts = refs[4 * n + 6 : 5 * n + 6]
    (
        sums, token_part, grad_part, hidden, both_grad, gate_rows, up_rows, back_rows,
        x_v, g_v, xe_v, ge_v,
    ) = refs[5 * n + 6 :]
    half, rows, wide = own[0][0].shape
    width = wide - LANES
    _, y, core = place_of(where)

    def fetch(tokens, grads):
        for t in range(n):
            span = slice(t * rows, (t + 1) * rows)
            of_x = [tokens[t][s // half].at[s % half] for s in range(n)]
            of_g = [grads[s][t // half].at[t % half] for s in range(n)]
            for s in range(n):
                x_v[span, s * width : (s + 1) * width] = of_x[s][:, :width]
                g_v[span, s * width : (s + 1) * width] = of_g[s][:, :width]
            xe_v[span] = sum(r[:, width:].astype(F32) for r in of_x)
            ge_v[span] = sum(r[:, width:].astype(F32) for r in of_g)
            token_part[(y - t + n) % n] = of_x[0][...]
            grad_part[(y - t + n) % n] = of_g[0][...]

    @pl.when(core == 0)
    def _():
        fetch(own, far)

    @pl.when(core != 0)
    def _():
        fetch(far, own)

    total = n * rows
    extra = xe_v[...]
    lane = lanes_of((total, LANES))
    tenant = jnp.sum(jnp.where(lane == 4 * RANK, extra, 0.0), axis=1, keepdims=True) / n
    mask = jnp.where((lane // RANK + 1).astype(F32) == tenant, 1.0, 0.0)
    row1 = rows_of((LANES, LANES))
    lane1 = lanes_of((LANES, LANES))
    spread = [onehot(row1 == lane1 % RANK + k * RANK) for k in range(2)]
    whole = (extra + pltpu.roll(extra, LANES - 2 * RANK, 1)).astype(BF)
    gate_adapter = (mask * dot(whole, spread[0])).astype(BF)
    up_adapter = (mask * dot(whole, spread[1])).astype(BF)
    extra = ge_v[...]
    whole = (extra + pltpu.roll(extra, LANES - RANK, 1)).astype(BF)
    back_adapter = (mask * dot(whole, spread[0])).astype(BF)
    gate_rows[...] = gate_adapter
    up_rows[...] = up_adapter
    back_rows[...] = back_adapter

    tokens = x_v[...]
    gate = dot(tokens, gate_w[...]) + SCALE * dot(gate_adapter, up_maps[0, 0])
    up = dot(tokens, up_w[...]) + SCALE * dot(up_adapter, up_maps[0, 1])
    sigmoid = jax.nn.sigmoid(gate)
    activated = gate * sigmoid
    state = (activated * up).astype(BF)
    hidden[...] = state
    grad_hidden = dot(g_v[...], down_t[...]) + SCALE * dot(
        back_adapter, out_down[0], ((1,), (1,))
    )
    grad_gate = (grad_hidden * up * sigmoid * (1.0 + gate * (1.0 - sigmoid))).astype(BF)
    grad_up = (grad_hidden * activated).astype(BF)
    columns = grad_gate.shape[1]
    both_grad[:, :columns] = grad_gate
    both_grad[:, columns:] = grad_up
    for s in range(n):
        result = dot(state, down_w[s]).astype(BF)
        for t in range(n):
            parts[t][s] = result[t * rows : (t + 1) * rows]

    pieces = [
        two_parts(mask * v)
        for v in (
            dot(state, out_down[0]),
            dot(grad_gate, up_maps[0, 0], ((1,), (1,))),
            dot(grad_up, up_maps[0, 1], ((1,), (1,))),
        )
    ]

    def moved(value, offset):
        return dot(value, onehot(lane1 - offset == row1 % RANK))

    value = jnp.zeros((total, LANES), F32)
    for k, (high, low) in enumerate(pieces):
        value += moved(high, k * RANK) + moved(low, (k + 3) * RANK)
    value = value.astype(BF)
    for t in range(n):
        sums[(y - t + n) % n] = value[t * rows : (t + 1) * rows]


def back_kernel(j, where, part, both_grad, both_t, sums, keep, send):
    n, rows, width = part.shape
    result = dot(both_grad[...], both_t[j]).astype(BF)

    def stored(output, gradient):
        for i in range(n):
            output[i, :, :width] = part[i]
            gradient[i, :, :width] = result[i * rows : (i + 1) * rows]
            output[i, :, width:] = sums[i]
            gradient[i, :, width:] = sums[i]

    @pl.when(where[2] == 0)
    def _():
        stored(keep, send)

    @pl.when(where[2] != 0)
    def _():
        stored(send, keep)


def hidden_grad_kernel(
    hidden, both_grad, gate_rows, up_rows, back_rows, input_up_grad, output_down_grad
):
    columns = hidden.shape[1]
    dims = ((0,), (0,))
    output_down_grad[0] = SCALE * dot(hidden[...], back_rows[...], dims)
    input_up_grad[0, 0] = SCALE * dot(gate_rows[...], both_grad[:, :columns], dims)
    input_up_grad[0, 1] = SCALE * dot(up_rows[...], both_grad[:, columns:], dims)


def joined_extra(pieces):
    value = sum(p.astype(F32) for p in pieces)
    lane = lanes_of(value.shape)
    width = 3 * RANK
    whole = value + pltpu.roll(value, LANES - width, 1)
    whole = jnp.where(lane < width, whole, 0.0)
    high, low = two_parts(whole)
    return (high.astype(F32) + pltpu.roll(low.astype(F32), width, 1)).astype(BF)


def joined(arrays):
    width = arrays[0].shape[1] - LANES
    main = sum(a[:, :width].astype(F32) for a in arrays).astype(BF)
    return main, joined_extra([a[:, width:] for a in arrays])


def pair_kernel(mine, theirs, out):
    for i in range(out.shape[0]):
        main, extra = joined([mine[i], theirs[i]])
        out[i, :, : main.shape[1]] = main
        out[i, :, main.shape[1] :] = extra


def first_kernel(mine, theirs, near1, near2, near3, *outs):
    for i, out_i in enumerate(outs):
        main, extra = joined([a[i] for a in (mine, theirs, near1, near2, near3)])
        width = main.shape[1]
        out_i[:, :width] = main
        for out in outs:
            out[:, width + i * LANES : width + (i + 1) * LANES] = extra


def tenants_of(part, width):
    extra = part[:, width:].astype(F32)
    lane = lanes_of(extra.shape)
    tenant = jnp.sum(jnp.where(lane == 4 * RANK, extra, 0.0), axis=1, keepdims=True)
    return jnp.where((lane // RANK + 1).astype(F32) == tenant, 1.0, 0.0)


def last_kernel(
    where, mine, near1, near2, near3, token_part, down_maps, up_map,
    keep, send, down_rows, up_rows,
):
    arrays = (mine, near1, near2, near3)
    n = len(arrays)
    rows, width = mine.shape[0], keep.shape[1]
    half = rows // 2
    _, y, core = place_of(where)
    row1 = rows_of((LANES, LANES))
    lane1 = lanes_of((LANES, LANES))
    spread = [onehot(row1 == lane1 % RANK + k * RANK) for k in range(3)]
    for i in range(n):
        at = width + i * LANES
        value = sum(a[:, at : at + LANES].astype(F32) for a in arrays)
        whole = (value + pltpu.roll(value, LANES - 3 * RANK, 1)).astype(BF)
        mask = tenants_of(token_part[i], width)
        down_rows[i] = (mask * dot(whole, spread[0])).astype(BF)
        up_rows[i, :, :LANES] = (mask * dot(whole, spread[1])).astype(BF)
        up_rows[i, :, LANES:] = (mask * dot(whole, spread[2])).astype(BF)
    value = sum(a[:, :width].astype(F32) for a in arrays)

    @pl.when(core == 0)
    def _():
        result = (value + SCALE * dot(down_rows[y], up_map[0])).astype(BF)
        keep[...] = result[:half]
        send[...] = result[half:]

    @pl.when(core != 0)
    def _():
        result = (value + SCALE * dot(up_rows[y], down_maps[0], ((1,), (1,)))).astype(BF)
        keep[...] = result[half:]
        send[...] = result[:half]


def adapter_grad_kernel(token_part, grad_part, down_rows, up_rows, input_down_grad, output_up_grad):
    n, _, _ = token_part.shape
    width = output_up_grad.shape[2]
    join = lambda ref, columns: jnp.concatenate([ref[i, :, :columns] for i in range(n)], axis=0)
    down = join(down_rows, LANES)
    up = join(up_rows, 2 * LANES)
    output_up_grad[0] = SCALE * dot(down, join(grad_part, width), ((0,), (0,)))
    input_down_grad[0] = SCALE * dot(join(token_part, width), up, ((0,), (0,)))


def return_kernel(mine, theirs, out):
    n_out, n = out.shape[0], mine.shape[0]
    row = rows_of((n_out, n))
    column = lanes_of((n_out, n))
    slot = row % GROUP
    base = (row // GROUP) * SLOTS
    first = onehot((slot < SLOTS) & (column == base + slot))
    second = onehot(
        (slot >= SLOTS) & (slot < 2 * SLOTS) & (column == base + slot - SLOTS)
    )
    out[...] = (dot(first, mine[...]) + dot(second, theirs[...])).astype(BF)


def combine_kernel(where, ids, logits, arrived, mixed, input_grad):
    n_in = arrived.shape[0]
    n_rows = mixed.shape[0]
    core = where[2]
    shift = core * SLOTS
    first, second = gates(logits[...])
    row = rows_of((n_rows, n_in))
    lane = lanes_of((n_rows, n_in))
    zero = jnp.zeros((n_rows, n_in), F32)
    picks = [[zero, zero], [zero, zero]]
    for t, k, expert, position in codes_of(ids):
        base = expert * GROUP + position
        picks[0][k] = jnp.where((row == t) & (lane == base + shift), 1.0, picks[0][k])
        picks[1][k] = jnp.where(
            (row == t) & (lane == base + SLOTS - shift), 1.0, picks[1][k]
        )
    data = arrived[...]
    value = [[dot(p.astype(BF), data) for p in pair] for pair in picks]
    mixed[...] = (first * value[0][0] + second * value[0][1]).astype(BF)
    input_grad[...] = (value[1][0] + value[1][1]).astype(BF)


def shape(dims, dtype=BF):
    return jax.ShapeDtypeStruct(tuple(dims), dtype)


def held(dims, dtype=BF):
    return pltpu.VMEM(tuple(dims), dtype)


def near_by(value):
    return pltpu.with_memory_space_constraint(value, pltpu.VMEM)


def far_off(value):
    return pltpu.with_memory_space_constraint(value, pltpu.HBM)


def per_device(
    tokens,
    out_grad,
    expert_ids,
    tenant_ids,
    router_logits,
    gate_projection_weight,
    up_projection_weight,
    down_projection_weight,
    input_down_maps,
    input_up_maps,
    output_down_map,
    output_up_map,
):
    n_experts = lax.axis_size("expert")
    n_data = lax.axis_size("dp")
    n = lax.axis_size("ffn")
    n_rows, width = tokens.shape
    hidden = gate_projection_weight.shape[2]
    columns = output_down_map.shape[2]
    slots = SLOTS * n_experts
    pair = 2 * slots
    wide = width + LANES
    plane = ("dp", "ffn")
    data_index = lax.axis_index("dp")
    where = jnp.stack([lax.axis_index("ffn"), data_index // 2, data_index % 2]).astype(I32)

    def turn(distance, stage):
        pairs = []
        for chip in range(n):
            for core in range(2):
                for split in range(n):
                    if core == stage:
                        to = (chip, (split + distance) % n)
                    else:
                        to = ((chip + distance) % n, split)
                    pairs.append(
                        ((2 * chip + core) * n + split, (2 * to[0] + core) * n + to[1])
                    )
        return pairs

    def turned(value, distance, stage):
        return lax.ppermute(value, plane, turn(distance, stage))

    def swapped(value):
        return lax.ppermute(value, "dp", [(i, i ^ 1) for i in range(n_data)])

    def call(kernel, out, *inputs, scalars=0, plain=0, scratch=(), limit=8):
        several = isinstance(out, list)
        return pl.pallas_call(
            kernel,
            out_shape=out,
            in_specs=[smem()] * scalars + [vmem()] * (len(inputs) - scalars),
            out_specs=[vmem()] * len(out) if several else vmem(),
            scratch_shapes=scratch,
            compiler_params=pltpu.CompilerParams(vmem_limit_bytes=limit * 1024 * 1024),
        )(*[far_off(v) if plain else v for v in inputs[: scalars + plain]], *[near_by(v) for v in inputs[scalars + plain :]])

    ids, logits = expert_ids.T, router_logits.T
    sent = call(
        dispatch_kernel, held((n_experts * GROUP, width)),
        ids, tenant_ids, logits, tokens, out_grad, scalars=2, plain=3,
    )
    arrived = lax.all_to_all(
        sent.reshape(n_experts, GROUP, width), "expert", 0, 0, tiled=True
    ).reshape(n_experts * GROUP, width)

    def loaded(kernel, out, *inputs, scalars=0, near=0):
        last = len(inputs) - near
        return pl.pallas_call(
            kernel,
            out_shape=out,
            in_specs=[smem()] * scalars + [anywhere()] * (last - scalars) + [vmem()] * near,
            out_specs=[vmem()] * len(out),
            scratch_shapes=[pltpu.SemaphoreType.DMA],
            compiler_params=pltpu.CompilerParams(vmem_limit_bytes=1024 * 1024),
        )(
            *inputs[:scalars],
            *[far_off(v) for v in inputs[scalars:last]],
            *[near_by(v) for v in inputs[last:]],
        )

    down_maps, up_map = loaded(
        maps_kernel,
        [held(input_down_maps.shape), held(output_up_map.shape)],
        input_down_maps, output_up_map,
    )
    keep, send = call(
        received_kernel, [held((slots, wide)), held((slots, wide))],
        where, arrived, down_maps, up_map, scalars=1,
    )
    other = swapped(send)
    unit = call(unit_kernel, held((pair, wide)), where, keep, other, scalars=1)
    line = [unit] + [turned(unit, s, 0) for s in range(1, n)]
    weights = loaded(
        weights_kernel,
        [held((n * width, hidden)), held((n * width, hidden)), held((n, hidden, width))],
        where, gate_projection_weight, up_projection_weight, down_projection_weight, unit,
        scalars=1, near=1,
    )
    crossed = [held((n, 2 * hidden, width)), held((n * width, hidden))]
    line_b = call(stack_kernel, held((2, pair, wide)), *line[2:], weights[2])
    line_a = call(stack_kernel, held((2, pair, wide)), *line[:2])
    near_a, far_b = turned(line_a, 1, 1), turned(line_b, n - 1, 1)
    near_b, far_a = turned(line_b, 1, 1), turned(line_a, n - 1, 1)
    near_a, far_b, *weights = lax.optimization_barrier((near_a, far_b, *weights))
    crossed = call(turned_weights_kernel, crossed, *weights)
    past_a, past_b = turned(near_a, 1, 1), turned(far_b, n - 1, 1)
    near_b, far_a, *crossed = lax.optimization_barrier((near_b, far_a, *crossed))
    own = [line_a, line_b, near_a, near_b, past_a, past_b, far_a, far_b]
    far = [swapped(v) for v in own]

    block = held((n, pair, wide))
    total = n * pair
    *parts, sums, token_part, grad_part, state, both_grad, gate_rows, up_rows, back_rows = call(
        expert_kernel,
        [held((n, pair, width))] * n
        + [
            held((n, pair, LANES)),
            block,
            block,
            held((total, hidden)),
            held((total, 2 * hidden)),
            held((total, columns)),
            held((total, columns)),
            held((total, columns)),
        ],
        where, *own, *far, *weights, crossed[1], input_up_maps, output_down_map,
        scalars=1,
        scratch=[
            pltpu.VMEM((total, n * width), BF),
            pltpu.VMEM((total, n * width), BF),
            pltpu.VMEM((total, LANES), F32),
            pltpu.VMEM((total, LANES), F32),
        ],
        limit=20,
    )
    keeps, theirs = {}, {}

    def reduced(j):
        keeps[j], send = call(
            functools.partial(back_kernel, j), [block, block],
            where, parts[j], both_grad, crossed[0], sums, scalars=1,
        )
        theirs[j] = swapped(send)

    def summed(j):
        return call(pair_kernel, block, keeps[j], theirs[j])

    for j in (2, 1, 3, 0):
        reduced(j)
    near = {j: turned(summed(j), n - j, 1) for j in (2, 1, 3)}
    input_up_gradient, output_down_gradient = call(
        hidden_grad_kernel,
        [shape((1, 2, columns, hidden), F32), shape((1, hidden, columns), F32)],
        state, both_grad, gate_rows, up_rows, back_rows,
    )
    tail = held((pair, width + n * LANES))
    lines = call(
        first_kernel, [tail] * n, keeps[0], theirs[0], near[1], near[2], near[3]
    )
    near = [turned(lines[j], n - j, 0) for j in range(1, n)]
    keep, send, down_rows, up_rows = call(
        last_kernel,
        [
            held((slots, width)),
            held((slots, width)),
            held((n, pair, columns)),
            held((n, pair, 2 * columns)),
        ],
        where, lines[0], *near, token_part, input_down_maps, output_up_map, scalars=1,
    )
    other = swapped(send)
    back = call(return_kernel, held((n_experts * GROUP, width)), keep, other)
    back = lax.all_to_all(
        back.reshape(n_experts, GROUP, width), "expert", 0, 0, tiled=True
    ).reshape(n_experts * GROUP, width)
    input_down_gradient, output_up_gradient = call(
        adapter_grad_kernel,
        [shape((1, width, 2 * columns), F32), shape((1, columns, width), F32)],
        token_part, grad_part, down_rows, up_rows,
    )
    mixed, input_grad = call(
        combine_kernel, [shape((n_rows, width)), shape((n_rows, width))],
        where, ids, logits, back, scalars=2,
    )
    return (
        mixed,
        input_grad,
        input_down_gradient,
        input_up_gradient,
        output_down_gradient,
        output_up_gradient,
    )


def solution(mesh):
    return jax.shard_map(
        per_device,
        mesh=mesh,
        in_specs=(
            P(("dp", "expert"), "ffn"),
            P(("dp", "expert"), "ffn"),
            P(("dp", "expert"), None),
            P(("dp", "expert")),
            P(("dp", "expert"), None),
            P("expert", None, ("dp", "ffn")),
            P("expert", None, ("dp", "ffn")),
            P("expert", ("dp", "ffn"), None),
            P("expert", "ffn", None),
            P("expert", None, None, ("dp", "ffn")),
            P("expert", ("dp", "ffn"), None),
            P("expert", None, "ffn"),
        ),
        out_specs=(
            P(("dp", "expert"), "ffn"),
            P(("dp", "expert"), "ffn"),
            P("expert", "ffn", None),
            P("expert", None, None, ("dp", "ffn")),
            P("expert", ("dp", "ffn"), None),
            P("expert", None, "ffn"),
        ),
        check_vma=False,
    )
```

profile of v0, /device:TPU:1, one launch (start us, length us, event | category | flops | bytes accessed | tf_op | source)
XLA Modules:
  0.0 120.2 jit_solution(14822063964903856531)
XLA Ops:
  0.6 1.9 %shard_map.163 = bf16[64,1536]{1,0:T(8,128)(2,1)} custom-call(s32[2,8]{1,0:T(2,128)} %bitcast.11, s32[8]{0:T(128)} %tenants.1, f32[2,8]{1,0:T(2,128)} %bitcast.13, bf16[8,1536]{1,0:T(8,128)(2,1)} %tokens.1, bf16[8,1536]{1,0:T(8,128)(2,1)} %grads.1), custom_call_target="tpu_custom_call" | custom-call | tf_op jit(solution)/shard_map/pallas_call | solution.py:523
  2.6 9.0 %all-to-all-start = ((bf16[8,8,1536]{2,1,0:T(8,128)(2,1)}), bf16[8,8,1536]{2,1,0:T(8,128)(2,1)S(1)}, u32[]{:S(2)}, u32[]{:S(2)}) async-start(bf16[8,8,1536]{2,1,0:T(8,128)(2,1)} %bitcast.5), calls=%async_computation | async-start | bytes 393216 | tf_op jit(solution)/shard_map/all_to_all | solution.py:537
  11.6 1.2 %shard_map.164 = (bf16[1,1536,256]{2,1,0:T(8,128)(2,1)S(1)}, bf16[1,128,1536]{2,1,0:T(8,128)(2,1)S(1)}) custom-call(bf16[1,1536,256]{2,1,0:T(8,128)(2,1)} %down_maps.3, bf16[1,128,1536]{2,1,0:T(8,128)(2,1)} %up_map.3), custom_call_target="tpu_custom_call" | custom-call | tf_op jit(solution)/shard_map/pallas_call | solution.py:543
  12.9 7.7 %all-to-all-done = bf16[8,8,1536]{2,1,0:T(8,128)(2,1)S(1)} async-done(((bf16[8,8,1536]{2,1,0:T(8,128)(2,1)}), bf16[8,8,1536]{2,1,0:T(8,128)(2,1)S(1)}, u32[]{:S(2)}, u32[]{:S(2)}) %all-to-all-start) | async-done | bytes 196640 | tf_op jit(solution)/shard_map/all_to_all | solution.py:537
  21.8 2.5 %collective-permute-start = (bf16[24,1664]{1,0:T(8,128)(2,1)S(1)}, bf16[24,1664]{1,0:T(8,128)(2,1)S(1)}, u32[]{:S(2)}, u32[]{:S(2)}) collective-permute-start(bf16[24,1664]{1,0:T(8,128)(2,1)S(1)} %get-tuple-element.61), channel_id=1, source_target_pairs={{0,32},{32,0},{64,96},{96,64},{128,160},{160,128},{192,224},{224,1... | collective-permute-start | bytes 239624 | tf_op jit(solution)/shard_map/ppermute | solution.py:519
  25.7 1.4 %collective-permute-start.1 = (bf16[48,1664]{1,0:T(8,128)(2,1)S(1)}, bf16[48,1664]{1,0:T(8,128)(2,1)S(1)}, u32[]{:S(2)}, u32[]{:S(2)}) collective-permute-start(bf16[48,1664]{1,0:T(8,128)(2,1)S(1)} %shard_map.166.first._), channel_id=1, source_target_pairs={{0,1},{1,2},{2,3},{3,0},{32,96},{33,97},{34,98},{35,99},{64,65},{6... | collective-permute-start | bytes 479240 | tf_op jit(solution)/shard_map/ppermute | solution.py:516
  27.1 1.5 %collective-permute-start.3 = (bf16[48,1664]{1,0:T(8,128)(2,1)S(1)}, bf16[48,1664]{1,0:T(8,128)(2,1)S(1)}, u32[]{:S(2)}, u32[]{:S(2)}) collective-permute-start(bf16[48,1664]{1,0:T(8,128)(2,1)S(1)} %shard_map.166.first._), channel_id=1, source_target_pairs={{0,3},{1,0},{2,1},{3,2},{32,224},{33,225},{34,226},{35,227},{64,67... | collective-permute-start | bytes 479240 | tf_op jit(solution)/shard_map/ppermute | solution.py:516
  28.6 1.6 %collective-permute-start.2 = (bf16[48,1664]{1,0:T(8,128)(2,1)S(1)}, bf16[48,1664]{1,0:T(8,128)(2,1)S(1)}, u32[]{:S(2)}, u32[]{:S(2)}) collective-permute-start(bf16[48,1664]{1,0:T(8,128)(2,1)S(1)} %shard_map.166.first._), channel_id=1, source_target_pairs={{0,2},{1,3},{2,0},{3,1},{32,160},{33,161},{34,162},{35,163},{64,66... | collective-permute-start | bytes 479240 | tf_op jit(solution)/shard_map/ppermute | solution.py:516
  30.2 4.3 %shard_map.168 = (bf16[6144,256]{1,0:T(8,128)(2,1)S(1)}, bf16[6144,256]{1,0:T(8,128)(2,1)S(1)}, bf16[4,256,1536]{2,1,0:T(8,128)(2,1)S(1)}) custom-call(s32[3]{0:T(128)S(1)} %pad_add_fusion.where, bf16[1,6144,256]{2,1,0:T(8,128)(2,1)} %gate_w.1, bf16[1,6144,256]{2,1,0:T(8,128)(2,1)} %up_w.1, bf16[1,256,6144]{2,1,0:T(8,128)(2,1)} %down_w.1, ...), custom_call_target="tpu_custom_call" | custom-call | tf_op jit(solution)/shard_map/pallas_call | solution.py:543
  34.6 1.3 %collective-permute-start.4 = (bf16[2,48,1664]{2,1,0:T(8,128)(2,1)S(1)}, bf16[2,48,1664]{2,1,0:T(8,128)(2,1)S(1)}, u32[]{:S(2)}, u32[]{:S(2)}) collective-permute-start(bf16[2,48,1664]{2,1,0:T(8,128)(2,1)S(1)} %shard_map.167.refs_0_), channel_id=1, source_target_pairs={{0,64},{1,65},{2,66},{3,67},{32,33},{33,34},{34,35},{35,32},{64,12... | collective-permute-start | bytes 958472 | tf_op jit(solution)/shard_map/ppermute | solution.py:516
  35.9 1.5 %collective-permute-start.5 = (bf16[2,48,1664]{2,1,0:T(8,128)(2,1)S(1)}, bf16[2,48,1664]{2,1,0:T(8,128)(2,1)S(1)}, u32[]{:S(2)}, u32[]{:S(2)}) collective-permute-start(bf16[2,48,1664]{2,1,0:T(8,128)(2,1)S(1)} %shard_map.169.refs_1_), channel_id=1, source_target_pairs={{0,192},{1,193},{2,194},{3,195},{32,35},{33,32},{34,33},{35,34},{6... | collective-permute-start | bytes 958472 | tf_op jit(solution)/shard_map/ppermute | solution.py:516
  37.4 1.3 %collective-permute-start.7 = (bf16[2,48,1664]{2,1,0:T(8,128)(2,1)S(1)}, bf16[2,48,1664]{2,1,0:T(8,128)(2,1)S(1)}, u32[]{:S(2)}, u32[]{:S(2)}) collective-permute-start(bf16[2,48,1664]{2,1,0:T(8,128)(2,1)S(1)} %shard_map.167.refs_0_), channel_id=1, source_target_pairs={{0,192},{1,193},{2,194},{3,195},{32,35},{33,32},{34,33},{35,34},{6... | collective-permute-start | bytes 958472 | tf_op jit(solution)/shard_map/ppermute | solution.py:516
  38.9 2.5 %collective-permute-start.10 = (bf16[2,48,1664]{2,1,0:T(8,128)(2,1)S(1)}, bf16[2,48,1664]{2,1,0:T(8,128)(2,1)S(1)}, u32[]{:S(2)}, u32[]{:S(2)}) collective-permute-start(bf16[2,48,1664]{2,1,0:T(8,128)(2,1)S(1)} %shard_map.167.refs_0_), channel_id=1, source_target_pairs={{0,32},{32,0},{64,96},{96,64},{128,160},{160,128},{192,224},{224,1... | collective-permute-start | bytes 958472 | tf_op jit(solution)/shard_map/ppermute | solution.py:519
  42.0 1.9 %collective-permute-start.11 = (bf16[2,48,1664]{2,1,0:T(8,128)(2,1)S(1)}, bf16[2,48,1664]{2,1,0:T(8,128)(2,1)S(1)}, u32[]{:S(2)}, u32[]{:S(2)}) collective-permute-start(bf16[2,48,1664]{2,1,0:T(8,128)(2,1)S(1)} %shard_map.169.refs_1_), channel_id=1, source_target_pairs={{0,32},{32,0},{64,96},{96,64},{128,160},{160,128},{192,224},{224,1... | collective-permute-start | bytes 958472 | tf_op jit(solution)/shard_map/ppermute | solution.py:519
  46.7 1.5 %collective-permute-start.9 = (bf16[2,48,1664]{2,1,0:T(8,128)(2,1)S(1)}, bf16[2,48,1664]{2,1,0:T(8,128)(2,1)S(1)}, u32[]{:S(2)}, u32[]{:S(2)}) collective-permute-start(bf16[2,48,1664]{2,1,0:T(8,128)(2,1)S(1)} %collective-permute-done.5.refs_7_), channel_id=1, source_target_pairs={{0,192},{1,193},{2,194},{3,195},{32,35},{33,32},{34,33},{35,34},{6... | collective-permute-start | bytes 958472 | tf_op jit(solution)/shard_map/ppermute | solution.py:516
  48.2 2.5 %shard_map.170 = (bf16[4,512,1536]{2,1,0:T(8,128)(2,1)S(1)}, bf16[6144,256]{1,0:T(8,128)(2,1)S(1)}) custom-call(bf16[6144,256]{1,0:T(8,128)(2,1)S(1)} %get-tuple-element.66.gate_v.refs_16_, bf16[6144,256]{1,0:T(8,128)(2,1)S(1)} %get-tuple-element.67.up_v.refs_17_, bf16[4,256,1536]{2,1,0:T(8,128)(2,1)S(1)} %get-tuple-element.68.rest_0_.down_v.refs_18_), custom_call_target="tpu_custom_call" | custom-call | tf_op jit(solution)/shard_map/pallas_call | solution.py:523
  50.7 3.1 %collective-permute-start.17 = (bf16[2,48,1664]{2,1,0:T(8,128)(2,1)S(1)}, bf16[2,48,1664]{2,1,0:T(8,128)(2,1)S(1)}, u32[]{:S(2)}, u32[]{:S(2)}) collective-permute-start(bf16[2,48,1664]{2,1,0:T(8,128)(2,1)S(1)} %collective-permute-done.5.refs_7_), channel_id=1, source_target_pairs={{0,32},{32,0},{64,96},{96,64},{128,160},{160,128},{192,224},{224,1... | collective-permute-start | bytes 958472 | tf_op jit(solution)/shard_map/ppermute | solution.py:519
  54.3 1.7 %collective-permute-start.14 = (bf16[2,48,1664]{2,1,0:T(8,128)(2,1)S(1)}, bf16[2,48,1664]{2,1,0:T(8,128)(2,1)S(1)}, u32[]{:S(2)}, u32[]{:S(2)}) collective-permute-start(bf16[2,48,1664]{2,1,0:T(8,128)(2,1)S(1)} %collective-permute-done.8.refs_4_), channel_id=1, source_target_pairs={{0,32},{32,0},{64,96},{96,64},{128,160},{160,128},{192,224},{224,1... | collective-permute-start | bytes 958472 | tf_op jit(solution)/shard_map/ppermute | solution.py:519
  57.7 4.3 %shard_map.171 = (bf16[4,48,1536]{2,1,0:T(8,128)(2,1)S(1)}, bf16[4,48,1536]{2,1,0:T(8,128)(2,1)S(1)}, bf16[4,48,1536]{2,1,0:T(8,128)(2,1)S(1)}, bf16[4,48,1536]{...) custom-call(s32[3]{0:T(128)S(1)} %pad_add_fusion.where, ...), custom_call_target="tpu_custom_call" | custom-call | tf_op jit(solution)/shard_map/pallas_call | solution.py:523
  68.2 1.3 %collective-permute-start.20 = (bf16[4,48,1664]{2,1,0:T(8,128)(2,1)S(1)}, bf16[4,48,1664]{2,1,0:T(8,128)(2,1)S(1)}, u32[]{:S(2)}, u32[]{:S(2)}) collective-permute-start(bf16[4,48,1664]{2,1,0:T(8,128)(2,1)S(1)} %shard_map.174), channel_id=1, source_target_pairs={{0,192},{1,193},{2,194},{3,195},{32,35},{33,32},{34,33},{35,34},{6... | collective-permute-start | bytes 1916936 | tf_op jit(solution)/shard_map/ppermute | solution.py:516
  71.6 6.2 %collective-permute-done.20.near1 = bf16[4,48,1664]{2,1,0:T(8,128)(2,1)S(1)} collective-permute-done((bf16[4,48,1664]{2,1,0:T(8,128)(2,1)S(1)}, bf16[4,48,1664]{2,1,0:T(8,128)(2,1)S(1)}, u32[]{:S(2)}, u32[]{:S(2)}) %collective-permute-start.20) | collective-permute-done | bytes 639008 | tf_op jit(solution)/shard_map/ppermute | solution.py:516
  77.8 3.4 %collective-permute-done.22.near2 = bf16[4,48,1664]{2,1,0:T(8,128)(2,1)S(1)} collective-permute-done((bf16[4,48,1664]{2,1,0:T(8,128)(2,1)S(1)}, bf16[4,48,1664]{2,1,0:T(8,128)(2,1)S(1)}, u32[]{:S(2)}, u32[]{:S(2)}) %collective-permute-start.22) | collective-permute-done | bytes 639008 | tf_op jit(solution)/shard_map/ppermute | solution.py:516
  81.2 6.8 %collective-permute-done.24.near3 = bf16[4,48,1664]{2,1,0:T(8,128)(2,1)S(1)} collective-permute-done((bf16[4,48,1664]{2,1,0:T(8,128)(2,1)S(1)}, bf16[4,48,1664]{2,1,0:T(8,128)(2,1)S(1)}, u32[]{:S(2)}, u32[]{:S(2)}) %collective-permute-start.24) | collective-permute-done | bytes 639008 | tf_op jit(solution)/shard_map/ppermute | solution.py:516
  88.6 2.3 %collective-permute-start.25 = (bf16[48,2048]{1,0:T(8,128)(2,1)S(1)}, bf16[48,2048]{1,0:T(8,128)(2,1)S(1)}, u32[]{:S(2)}, u32[]{:S(2)}) collective-permute-start(bf16[48,2048]{1,0:T(8,128)(2,1)S(1)} %get-tuple-element.91), channel_id=1, source_target_pairs={{0,3},{1,0},{2,1},{3,2},{32,224},{33,225},{34,226},{35,227},{64,67... | collective-permute-start | bytes 589832 | tf_op jit(solution)/shard_map/ppermute | solution.py:516
  92.0 3.6 %collective-permute-done.25.near1 = bf16[48,2048]{1,0:T(8,128)(2,1)S(1)} collective-permute-done((bf16[48,2048]{1,0:T(8,128)(2,1)S(1)}, bf16[48,2048]{1,0:T(8,128)(2,1)S(1)}, u32[]{:S(2)}, u32[]{:S(2)}) %collective-permute-start.25) | collective-permute-done | bytes 196640 | tf_op jit(solution)/shard_map/ppermute | solution.py:516
  95.6 1.4 %collective-permute-done.26.near2 = bf16[48,2048]{1,0:T(8,128)(2,1)S(1)} collective-permute-done((bf16[48,2048]{1,0:T(8,128)(2,1)S(1)}, bf16[48,2048]{1,0:T(8,128)(2,1)S(1)}, u32[]{:S(2)}, u32[]{:S(2)}) %collective-permute-start.26) | collective-permute-done | bytes 196640 | tf_op jit(solution)/shard_map/ppermute | solution.py:516
  97.0 2.3 %collective-permute-done.27.near3 = bf16[48,2048]{1,0:T(8,128)(2,1)S(1)} collective-permute-done((bf16[48,2048]{1,0:T(8,128)(2,1)S(1)}, bf16[48,2048]{1,0:T(8,128)(2,1)S(1)}, u32[]{:S(2)}, u32[]{:S(2)}) %collective-permute-start.27) | collective-permute-done | bytes 196640 | tf_op jit(solution)/shard_map/ppermute | solution.py:516
  100.6 2.9 %collective-permute-start.28 = (bf16[24,1536]{1,0:T(8,128)(2,1)S(1)}, bf16[24,1536]{1,0:T(8,128)(2,1)S(1)}, u32[]{:S(2)}, u32[]{:S(2)}) collective-permute-start(bf16[24,1536]{1,0:T(8,128)(2,1)S(1)} %get-tuple-element.96), channel_id=1, source_target_pairs={{0,32},{32,0},{64,96},{96,64},{128,160},{160,128},{192,224},{224,1... | collective-permute-start | bytes 221192 | tf_op jit(solution)/shard_map/ppermute | solution.py:519
  105.3 3.4 %all-to-all-start.1 = ((bf16[8,8,1536]{2,1,0:T(8,128)(2,1)}), bf16[8,8,1536]{2,1,0:T(8,128)(2,1)S(1)}, u32[]{:S(2)}, u32[]{:S(2)}) async-start(bf16[8,8,1536]{2,1,0:T(8,128)(2,1)} %bitcast.7), calls=%async_computation.1 | async-start | bytes 393216 | tf_op jit(solution)/shard_map/all_to_all | solution.py:648
  109.7 1.7 %shard_map.183 = (f32[1,1536,256]{2,1,0:T(8,128)}, f32[1,128,1536]{2,1,0:T(8,128)}) custom-call(bf16[4,48,1664]{2,1,0:T(8,128)(2,1)S(1)} %get-tuple-element.94.token_part, bf16[4,48,1664]{2,1,0:T(8,128)(2,1)S(1)} %get-tuple-element.99.grad_part, bf16[4,48,128]{2,1,0:T(8,128)(2,1)S(1)} %get-tuple-element.100.down_rows, ...), custom_call_target="tpu_custom_call" | custom-call | tf_op jit(solution)/shard_map/pallas_call | solution.py:523
  111.4 7.3 %all-to-all-done.1 = bf16[8,8,1536]{2,1,0:T(8,128)(2,1)S(1)} async-done(((bf16[8,8,1536]{2,1,0:T(8,128)(2,1)}), bf16[8,8,1536]{2,1,0:T(8,128)(2,1)S(1)}, u32[]{:S(2)}, u32[]{:S(2)}) %all-to-all-start.1) | async-done | bytes 196640 | tf_op jit(solution)/shard_map/all_to_all | solution.py:648
  118.7 1.5 %shard_map.182 = (bf16[8,1536]{1,0:T(8,128)(2,1)}, bf16[8,1536]{1,0:T(8,128)(2,1)}) custom-call(s32[3]{0:T(128)S(1)} %pad_add_fusion.where, s32[2,8]{1,0:T(2,128)S(1)} %bitcast.12, f32[2,8]{1,0:T(2,128)S(1)} %bitcast.14, bf16[64,1536]{1,0:T(8,128)(2,1)S(1)} %bitcast.10), custom_call_target="tpu_custom_call" | custom-call | tf_op jit(solution)/shard_map/pallas_call | solution.py:523
  (65 shorter events, 22.9 us)
Async XLA Ops:
  2.6 18.0 %all-to-all-start = ((bf16[8,8,1536]{2,1,0:T(8,128)(2,1)}), bf16[8,8,1536]{2,1,0:T(8,128)(2,1)S(1)}, u32[]{:S(2)}, u32[]{:S(2)}) async-start(bf16[8,8,1536]{2,1,0:T(8,128)(2,1)} %bitcast.5), calls=%async_computation | async-start | bytes 393216 | tf_op jit(solution)/shard_map/all_to_all | solution.py:537
  21.8 3.4 %collective-permute-start = (bf16[24,1664]{1,0:T(8,128)(2,1)S(1)}, bf16[24,1664]{1,0:T(8,128)(2,1)S(1)}, u32[]{:S(2)}, u32[]{:S(2)}) collective-permute-start(bf16[24,1664]{1,0:T(8,128)(2,1)S(1)} %get-tuple-element.61), channel_id=1, source_target_pairs={{0,32},{32,0},{64,96},{96,64},{128,160},{160,128},{192,224},{224,1... | collective-permute-start | bytes 239624 | tf_op jit(solution)/shard_map/ppermute | solution.py:519
  25.7 8.8 %collective-permute-start.1 = (bf16[48,1664]{1,0:T(8,128)(2,1)S(1)}, bf16[48,1664]{1,0:T(8,128)(2,1)S(1)}, u32[]{:S(2)}, u32[]{:S(2)}) collective-permute-start(bf16[48,1664]{1,0:T(8,128)(2,1)S(1)} %shard_map.166.first._), channel_id=1, source_target_pairs={{0,1},{1,2},{2,3},{3,0},{32,96},{33,97},{34,98},{35,99},{64,65},{6... | collective-permute-start | bytes 479240 | tf_op jit(solution)/shard_map/ppermute | solution.py:516
  27.1 8.7 %collective-permute-start.3 = (bf16[48,1664]{1,0:T(8,128)(2,1)S(1)}, bf16[48,1664]{1,0:T(8,128)(2,1)S(1)}, u32[]{:S(2)}, u32[]{:S(2)}) collective-permute-start(bf16[48,1664]{1,0:T(8,128)(2,1)S(1)} %shard_map.166.first._), channel_id=1, source_target_pairs={{0,3},{1,0},{2,1},{3,2},{32,224},{33,225},{34,226},{35,227},{64,67... | collective-permute-start | bytes 479240 | tf_op jit(solution)/shard_map/ppermute | solution.py:516
  28.6 7.2 %collective-permute-start.2 = (bf16[48,1664]{1,0:T(8,128)(2,1)S(1)}, bf16[48,1664]{1,0:T(8,128)(2,1)S(1)}, u32[]{:S(2)}, u32[]{:S(2)}) collective-permute-start(bf16[48,1664]{1,0:T(8,128)(2,1)S(1)} %shard_map.166.first._), channel_id=1, source_target_pairs={{0,2},{1,3},{2,0},{3,1},{32,160},{33,161},{34,162},{35,163},{64,66... | collective-permute-start | bytes 479240 | tf_op jit(solution)/shard_map/ppermute | solution.py:516
  34.6 7.4 %collective-permute-start.4 = (bf16[2,48,1664]{2,1,0:T(8,128)(2,1)S(1)}, bf16[2,48,1664]{2,1,0:T(8,128)(2,1)S(1)}, u32[]{:S(2)}, u32[]{:S(2)}) collective-permute-start(bf16[2,48,1664]{2,1,0:T(8,128)(2,1)S(1)} %shard_map.167.refs_0_), channel_id=1, source_target_pairs={{0,64},{1,65},{2,66},{3,67},{32,33},{33,34},{34,35},{35,32},{64,12... | collective-permute-start | bytes 958472 | tf_op jit(solution)/shard_map/ppermute | solution.py:516
  35.9 8.0 %collective-permute-start.5 = (bf16[2,48,1664]{2,1,0:T(8,128)(2,1)S(1)}, bf16[2,48,1664]{2,1,0:T(8,128)(2,1)S(1)}, u32[]{:S(2)}, u32[]{:S(2)}) collective-permute-start(bf16[2,48,1664]{2,1,0:T(8,128)(2,1)S(1)} %shard_map.169.refs_1_), channel_id=1, source_target_pairs={{0,192},{1,193},{2,194},{3,195},{32,35},{33,32},{34,33},{35,34},{6... | collective-permute-start | bytes 958472 | tf_op jit(solution)/shard_map/ppermute | solution.py:516
  37.4 8.1 %collective-permute-start.7 = (bf16[2,48,1664]{2,1,0:T(8,128)(2,1)S(1)}, bf16[2,48,1664]{2,1,0:T(8,128)(2,1)S(1)}, u32[]{:S(2)}, u32[]{:S(2)}) collective-permute-start(bf16[2,48,1664]{2,1,0:T(8,128)(2,1)S(1)} %shard_map.167.refs_0_), channel_id=1, source_target_pairs={{0,192},{1,193},{2,194},{3,195},{32,35},{33,32},{34,33},{35,34},{6... | collective-permute-start | bytes 958472 | tf_op jit(solution)/shard_map/ppermute | solution.py:516
  38.7 8.0 %collective-permute-start.6 = (bf16[2,48,1664]{2,1,0:T(8,128)(2,1)S(1)}, bf16[2,48,1664]{2,1,0:T(8,128)(2,1)S(1)}, u32[]{:S(2)}, u32[]{:S(2)}) collective-permute-start(bf16[2,48,1664]{2,1,0:T(8,128)(2,1)S(1)} %shard_map.169.refs_1_), channel_id=1, source_target_pairs={{0,64},{1,65},{2,66},{3,67},{32,33},{33,34},{34,35},{35,32},{64,12... | collective-permute-start | bytes 958472 | tf_op jit(solution)/shard_map/ppermute | solution.py:516
  38.9 11.8 %collective-permute-start.10 = (bf16[2,48,1664]{2,1,0:T(8,128)(2,1)S(1)}, bf16[2,48,1664]{2,1,0:T(8,128)(2,1)S(1)}, u32[]{:S(2)}, u32[]{:S(2)}) collective-permute-start(bf16[2,48,1664]{2,1,0:T(8,128)(2,1)S(1)} %shard_map.167.refs_0_), channel_id=1, source_target_pairs={{0,32},{32,0},{64,96},{96,64},{128,160},{160,128},{192,224},{224,1... | collective-permute-start | bytes 958472 | tf_op jit(solution)/shard_map/ppermute | solution.py:519
  42.0 11.8 %collective-permute-start.11 = (bf16[2,48,1664]{2,1,0:T(8,128)(2,1)S(1)}, bf16[2,48,1664]{2,1,0:T(8,128)(2,1)S(1)}, u32[]{:S(2)}, u32[]{:S(2)}) collective-permute-start(bf16[2,48,1664]{2,1,0:T(8,128)(2,1)S(1)} %shard_map.169.refs_1_), channel_id=1, source_target_pairs={{0,32},{32,0},{64,96},{96,64},{128,160},{160,128},{192,224},{224,1... | collective-permute-start | bytes 958472 | tf_op jit(solution)/shard_map/ppermute | solution.py:519
  43.9 10.0 %collective-permute-start.12 = (bf16[2,48,1664]{2,1,0:T(8,128)(2,1)S(1)}, bf16[2,48,1664]{2,1,0:T(8,128)(2,1)S(1)}, u32[]{:S(2)}, u32[]{:S(2)}) collective-permute-start(bf16[2,48,1664]{2,1,0:T(8,128)(2,1)S(1)} %collective-permute-done.4.refs_2_), channel_id=1, source_target_pairs={{0,32},{32,0},{64,96},{96,64},{128,160},{160,128},{192,224},{224,1... | collective-permute-start | bytes 958472 | tf_op jit(solution)/shard_map/ppermute | solution.py:519
  45.5 8.8 %collective-permute-start.8 = (bf16[2,48,1664]{2,1,0:T(8,128)(2,1)S(1)}, bf16[2,48,1664]{2,1,0:T(8,128)(2,1)S(1)}, u32[]{:S(2)}, u32[]{:S(2)}) collective-permute-start(bf16[2,48,1664]{2,1,0:T(8,128)(2,1)S(1)} %collective-permute-done.4.refs_2_), channel_id=1, source_target_pairs={{0,64},{1,65},{2,66},{3,67},{32,33},{33,34},{34,35},{35,32},{64,12... | collective-permute-start | bytes 958472 | tf_op jit(solution)/shard_map/ppermute | solution.py:516
  46.7 9.2 %collective-permute-start.9 = (bf16[2,48,1664]{2,1,0:T(8,128)(2,1)S(1)}, bf16[2,48,1664]{2,1,0:T(8,128)(2,1)S(1)}, u32[]{:S(2)}, u32[]{:S(2)}) collective-permute-start(bf16[2,48,1664]{2,1,0:T(8,128)(2,1)S(1)} %collective-permute-done.5.refs_7_), channel_id=1, source_target_pairs={{0,192},{1,193},{2,194},{3,195},{32,35},{33,32},{34,33},{35,34},{6... | collective-permute-start | bytes 958472 | tf_op jit(solution)/shard_map/ppermute | solution.py:516
  50.7 5.6 %collective-permute-start.17 = (bf16[2,48,1664]{2,1,0:T(8,128)(2,1)S(1)}, bf16[2,48,1664]{2,1,0:T(8,128)(2,1)S(1)}, u32[]{:S(2)}, u32[]{:S(2)}) collective-permute-start(bf16[2,48,1664]{2,1,0:T(8,128)(2,1)S(1)} %collective-permute-done.5.refs_7_), channel_id=1, source_target_pairs={{0,32},{32,0},{64,96},{96,64},{128,160},{160,128},{192,224},{224,1... | collective-permute-start | bytes 958472 | tf_op jit(solution)/shard_map/ppermute | solution.py:519
  53.8 2.6 %collective-permute-start.13 = (bf16[2,48,1664]{2,1,0:T(8,128)(2,1)S(1)}, bf16[2,48,1664]{2,1,0:T(8,128)(2,1)S(1)}, u32[]{:S(2)}, u32[]{:S(2)}) collective-permute-start(bf16[2,48,1664]{2,1,0:T(8,128)(2,1)S(1)} %collective-permute-done.6.refs_3_), channel_id=1, source_target_pairs={{0,32},{32,0},{64,96},{96,64},{128,160},{160,128},{192,224},{224,1... | collective-permute-start | bytes 958472 | tf_op jit(solution)/shard_map/ppermute | solution.py:519
  53.9 2.5 %collective-permute-start.16 = (bf16[2,48,1664]{2,1,0:T(8,128)(2,1)S(1)}, bf16[2,48,1664]{2,1,0:T(8,128)(2,1)S(1)}, u32[]{:S(2)}, u32[]{:S(2)}) collective-permute-start(bf16[2,48,1664]{2,1,0:T(8,128)(2,1)S(1)} %collective-permute-done.7.refs_6_), channel_id=1, source_target_pairs={{0,32},{32,0},{64,96},{96,64},{128,160},{160,128},{192,224},{224,1... | collective-permute-start | bytes 958472 | tf_op jit(solution)/shard_map/ppermute | solution.py:519
  54.3 2.9 %collective-permute-start.14 = (bf16[2,48,1664]{2,1,0:T(8,128)(2,1)S(1)}, bf16[2,48,1664]{2,1,0:T(8,128)(2,1)S(1)}, u32[]{:S(2)}, u32[]{:S(2)}) collective-permute-start(bf16[2,48,1664]{2,1,0:T(8,128)(2,1)S(1)} %collective-permute-done.8.refs_4_), channel_id=1, source_target_pairs={{0,32},{32,0},{64,96},{96,64},{128,160},{160,128},{192,224},{224,1... | collective-permute-start | bytes 958472 | tf_op jit(solution)/shard_map/ppermute | solution.py:519
  56.0 1.7 %collective-permute-start.15 = (bf16[2,48,1664]{2,1,0:T(8,128)(2,1)S(1)}, bf16[2,48,1664]{2,1,0:T(8,128)(2,1)S(1)}, u32[]{:S(2)}, u32[]{:S(2)}) collective-permute-start(bf16[2,48,1664]{2,1,0:T(8,128)(2,1)S(1)} %collective-permute-done.9.refs_5_), channel_id=1, source_target_pairs={{0,32},{32,0},{64,96},{96,64},{128,160},{160,128},{192,224},{224,1... | collective-permute-start | bytes 958472 | tf_op jit(solution)/shard_map/ppermute | solution.py:519
  63.1 4.8 %collective-permute-start.19 = (bf16[4,48,1664]{2,1,0:T(8,128)(2,1)S(1)}, bf16[4,48,1664]{2,1,0:T(8,128)(2,1)S(1)}, u32[]{:S(2)}, u32[]{:S(2)}) collective-permute-start(bf16[4,48,1664]{2,1,0:T(8,128)(2,1)S(1)} %get-tuple-element.83), channel_id=1, source_target_pairs={{0,32},{32,0},{64,96},{96,64},{128,160},{160,128},{192,224},{224,1... | collective-permute-start | bytes 1916936 | tf_op jit(solution)/shard_map/ppermute | solution.py:519
  64.7 4.8 %collective-permute-start.21 = (bf16[4,48,1664]{2,1,0:T(8,128)(2,1)S(1)}, bf16[4,48,1664]{2,1,0:T(8,128)(2,1)S(1)}, u32[]{:S(2)}, u32[]{:S(2)}) collective-permute-start(bf16[4,48,1664]{2,1,0:T(8,128)(2,1)S(1)} %get-tuple-element.86), channel_id=1, source_target_pairs={{0,32},{32,0},{64,96},{96,64},{128,160},{160,128},{192,224},{224,1... | collective-permute-start | bytes 1916936 | tf_op jit(solution)/shard_map/ppermute | solution.py:519
  66.1 4.9 %collective-permute-start.23 = (bf16[4,48,1664]{2,1,0:T(8,128)(2,1)S(1)}, bf16[4,48,1664]{2,1,0:T(8,128)(2,1)S(1)}, u32[]{:S(2)}, u32[]{:S(2)}) collective-permute-start(bf16[4,48,1664]{2,1,0:T(8,128)(2,1)S(1)} %get-tuple-element.89), channel_id=1, source_target_pairs={{0,32},{32,0},{64,96},{96,64},{128,160},{160,128},{192,224},{224,1... | collective-permute-start | bytes 1916936 | tf_op jit(solution)/shard_map/ppermute | solution.py:519
  67.7 3.9 %collective-permute-start.18 = (bf16[4,48,1664]{2,1,0:T(8,128)(2,1)S(1)}, bf16[4,48,1664]{2,1,0:T(8,128)(2,1)S(1)}, u32[]{:S(2)}, u32[]{:S(2)}) collective-permute-start(bf16[4,48,1664]{2,1,0:T(8,128)(2,1)S(1)} %get-tuple-element.80), channel_id=1, source_target_pairs={{0,32},{32,0},{64,96},{96,64},{128,160},{160,128},{192,224},{224,1... | collective-permute-start | bytes 1916936 | tf_op jit(solution)/shard_map/ppermute | solution.py:519
  68.2 9.6 %collective-permute-start.20 = (bf16[4,48,1664]{2,1,0:T(8,128)(2,1)S(1)}, bf16[4,48,1664]{2,1,0:T(8,128)(2,1)S(1)}, u32[]{:S(2)}, u32[]{:S(2)}) collective-permute-start(bf16[4,48,1664]{2,1,0:T(8,128)(2,1)S(1)} %shard_map.174), channel_id=1, source_target_pairs={{0,192},{1,193},{2,194},{3,195},{32,35},{33,32},{34,33},{35,34},{6... | collective-permute-start | bytes 1916936 | tf_op jit(solution)/shard_map/ppermute | solution.py:516
  69.8 11.4 %collective-permute-start.22 = (bf16[4,48,1664]{2,1,0:T(8,128)(2,1)S(1)}, bf16[4,48,1664]{2,1,0:T(8,128)(2,1)S(1)}, u32[]{:S(2)}, u32[]{:S(2)}) collective-permute-start(bf16[4,48,1664]{2,1,0:T(8,128)(2,1)S(1)} %shard_map.176), channel_id=1, source_target_pairs={{0,128},{1,129},{2,130},{3,131},{32,34},{33,35},{34,32},{35,33},{6... | collective-permute-start | bytes 1916936 | tf_op jit(solution)/shard_map/ppermute | solution.py:516
  71.3 16.7 %collective-permute-start.24 = (bf16[4,48,1664]{2,1,0:T(8,128)(2,1)S(1)}, bf16[4,48,1664]{2,1,0:T(8,128)(2,1)S(1)}, u32[]{:S(2)}, u32[]{:S(2)}) collective-permute-start(bf16[4,48,1664]{2,1,0:T(8,128)(2,1)S(1)} %shard_map.178), channel_id=1, source_target_pairs={{0,64},{1,65},{2,66},{3,67},{32,33},{33,34},{34,35},{35,32},{64,12... | collective-permute-start | bytes 1916936 | tf_op jit(solution)/shard_map/ppermute | solution.py:516
  88.6 30.1 %copy-start.4 = (s32[8,2]{0,1:T(2,128)S(1)}, s32[8,2]{0,1:T(2,128)}, u32[]{:S(2)}) copy-start(s32[8,2]{0,1:T(2,128)} %param.14) | copy-start | bytes 196
  88.6 7.0 %collective-permute-start.25 = (bf16[48,2048]{1,0:T(8,128)(2,1)S(1)}, bf16[48,2048]{1,0:T(8,128)(2,1)S(1)}, u32[]{:S(2)}, u32[]{:S(2)}) collective-permute-start(bf16[48,2048]{1,0:T(8,128)(2,1)S(1)} %get-tuple-element.91), channel_id=1, source_target_pairs={{0,3},{1,0},{2,1},{3,2},{32,224},{33,225},{34,226},{35,227},{64,67... | collective-permute-start | bytes 589832 | tf_op jit(solution)/shard_map/ppermute | solution.py:516
  90.9 6.1 %collective-permute-start.26 = (bf16[48,2048]{1,0:T(8,128)(2,1)S(1)}, bf16[48,2048]{1,0:T(8,128)(2,1)S(1)}, u32[]{:S(2)}, u32[]{:S(2)}) collective-permute-start(bf16[48,2048]{1,0:T(8,128)(2,1)S(1)} %get-tuple-element.92), channel_id=1, source_target_pairs={{0,2},{1,3},{2,0},{3,1},{32,160},{33,161},{34,162},{35,163},{64,66... | collective-permute-start | bytes 589832 | tf_op jit(solution)/shard_map/ppermute | solution.py:516
  91.3 8.1 %collective-permute-start.27 = (bf16[48,2048]{1,0:T(8,128)(2,1)S(1)}, bf16[48,2048]{1,0:T(8,128)(2,1)S(1)}, u32[]{:S(2)}, u32[]{:S(2)}) collective-permute-start(bf16[48,2048]{1,0:T(8,128)(2,1)S(1)} %get-tuple-element.93), channel_id=1, source_target_pairs={{0,1},{1,2},{2,3},{3,0},{32,96},{33,97},{34,98},{35,99},{64,65},{6... | collective-permute-start | bytes 589832 | tf_op jit(solution)/shard_map/ppermute | solution.py:516
  100.6 3.8 %collective-permute-start.28 = (bf16[24,1536]{1,0:T(8,128)(2,1)S(1)}, bf16[24,1536]{1,0:T(8,128)(2,1)S(1)}, u32[]{:S(2)}, u32[]{:S(2)}) collective-permute-start(bf16[24,1536]{1,0:T(8,128)(2,1)S(1)} %get-tuple-element.96), channel_id=1, source_target_pairs={{0,32},{32,0},{64,96},{96,64},{128,160},{160,128},{192,224},{224,1... | collective-permute-start | bytes 221192 | tf_op jit(solution)/shard_map/ppermute | solution.py:519
  105.3 13.4 %all-to-all-start.1 = ((bf16[8,8,1536]{2,1,0:T(8,128)(2,1)}), bf16[8,8,1536]{2,1,0:T(8,128)(2,1)S(1)}, u32[]{:S(2)}, u32[]{:S(2)}) async-start(bf16[8,8,1536]{2,1,0:T(8,128)(2,1)} %bitcast.7), calls=%async_computation.1 | async-start | bytes 393216 | tf_op jit(solution)/shard_map/all_to_all | solution.py:648
  (5 other events, 117.4 us)
where the time goes:
time: 121 us; the launch traced here: 120 us
  starting transfers between devices  47.2 us (39%)
  waiting for transfers between devices  43.6 us (36%)
  Pallas kernels  28.4 us (23%)
    ppermute x15, waiting for transfers between devices, turned(): return lax.ppermute(value, plane, turn(distance, stage))  25.5 us
    pallas_call x20, Pallas kernels, call(): pl.pallas_call(kernel, out_shape=out, in_specs=[smem()] * scalars + [vmem...  22.9 us
    ppermute x15, starting transfers between devices, turned(): return lax.ppermute(value, plane, turn(distance, stage))  17.6 us
    ppermute x14, starting transfers between devices, swapped(): return lax.ppermute(value, 'dp', [(i, i ^ 1) for i in range(n_data)])  17.2 us
    all_to_all x1, starting transfers between devices, per_device(): lax.all_to_all(sent.reshape(n_experts, GROUP, width), 'expert', 0, 0, til...  9.01 us
    all_to_all x1, waiting for transfers between devices, per_device(): lax.all_to_all(sent.reshape(n_experts, GROUP, width), 'expert', 0, 0, til...  7.67 us
    all_to_all x1, waiting for transfers between devices, per_device(): lax.all_to_all(back.reshape(n_experts, GROUP, width), 'expert', 0, 0, til...  7.28 us
    pallas_call x2, Pallas kernels, loaded(): pl.pallas_call(kernel, out_shape=out, in_specs=[smem()] * scalars + [anyw...  5.54 us
  transfers between devices with their start and end apart: 31, of which 14 were waited for; matrix products, arithmetic and copies ran while one was open for 0% of the time, Pallas kernels for 13%

commit v1 on v0

--- a/solution.py
+++ b/solution.py
@@ -77,45 +77,69 @@
 
 def dispatch_kernel(ids, tenants, logits, tokens, grads, out):
     n_out = out.shape[0]
-    n_rows = tokens.shape[0]
+    n_rows, width = tokens.shape
+    main = out.shape[1] - LANES
+    tail = width - main
     codes = codes_of(ids)
     first, second = gates(logits[...])
     row = rows_of((n_out, LANES))
     lane = lanes_of((n_out, LANES))
-    pick_token = jnp.zeros((n_out, LANES), F32)
-    pick_grad = jnp.zeros((n_out, LANES), F32)
+    slot, base = row % GROUP, row - row % GROUP
+    head = jnp.zeros((n_out, LANES), F32)
+    tails = [jnp.zeros((n_out, LANES), F32) for _ in range(SLOTS)]
     tenant_row = jnp.zeros((n_out, LANES), F32)
     for t, k, expert, position in codes:
-        base = expert * GROUP
-        pick_token = jnp.where((row == base + position) & (lane == t), 1.0, pick_token)
-        pick_grad = jnp.where(
-            (row == base + SLOTS + position) & (lane == t + k * n_rows), 1.0, pick_grad
-        )
+        here = base == expert * GROUP
+        as_token = lane == t
+        as_grad = lane == (1 + k) * n_rows + t
+        chosen = (as_token & (slot == position)) | (as_grad & (slot == SLOTS + position))
+        head = jnp.where(here & chosen, 1.0, head)
+        chosen = (as_token & (slot == 2 * SLOTS)) | (as_grad & (slot == 2 * SLOTS + 1))
+        for p in range(SLOTS):
+            tails[p] = jnp.where(here & chosen & (position == p), 1.0, tails[p])
         code = (tenants[t] + 1).astype(F32)
         tenant_row = jnp.where(
-            (row == base + 2 * SLOTS) & (lane == position), code, tenant_row
+            here & (slot == 2 * SLOTS) & (lane == position), code, tenant_row
         )
     g = grads[...].astype(F32)
-    scaled = jnp.concatenate([(first * g).astype(BF), (second * g).astype(BF)], axis=0)
-    value = dot(pick_token[:, :n_rows].astype(BF), tokens[...]) + dot(
-        pick_grad[:, : 2 * n_rows].astype(BF), scaled
-    )
-    out[...] = value.astype(BF)
-    out[:, :LANES] = (value[:, :LANES] + tenant_row).astype(BF)
+    source = jnp.concatenate(
+        [tokens[...], (first * g).astype(BF), (second * g).astype(BF)], axis=0
+    )
+    n_source = 3 * n_rows
+    value = dot(head[:, :n_source].astype(BF), source[:, :main])
+    out[:, :main] = value.astype(BF)
+    for p in range(SLOTS):
+        span = slice(p * tail, (p + 1) * tail)
+        value_p = dot(tails[p][:, :n_source].astype(BF), source[:, main:])
+        out[:, span] = (value[:, span] + value_p).astype(BF)
+    out[:, main:] = tenant_row.astype(BF)
 
 
 def received_kernel(where, arrived, down_maps, up_map, keep, send):
-    n_in, width = arrived.shape
-    n = keep.shape[0]
+    n_in = arrived.shape[0]
+    n, width = keep.shape[0], keep.shape[1] - LANES
+    main = arrived.shape[1] - LANES
+    tail = width - main
     core = where[2]
     row = rows_of((n, n_in))
     column = lanes_of((n, n_in))
     start = (row // SLOTS) * GROUP
     offset = row % SLOTS
     data = arrived[...]
-    tokens = dot(onehot(column == start + offset), data).astype(BF)
-    grads = dot(onehot(column == start + SLOTS + offset), data).astype(BF)
-    tenants = dot(onehot(column == start + 2 * SLOTS), data[:, :LANES])
+
+    def unpacked(kind):
+        head = dot(onehot(column == start + kind * SLOTS + offset), data[:, :main])
+        rest = sum(
+            dot(
+                onehot((column == start + 2 * SLOTS + kind) & (offset == p)),
+                data[:, p * tail : (p + 1) * tail],
+            )
+            for p in range(SLOTS)
+        )
+        return jnp.concatenate([head.astype(BF), rest.astype(BF)], axis=1)
+
+    tokens, grads = unpacked(0), unpacked(1)
+    tenants = dot(onehot(column == start + 2 * SLOTS), data[:, main:])
     lane = lanes_of((n, LANES))
     tenant = jnp.sum(
         jnp.where(lane == rows_of((n, LANES)) % SLOTS, tenants, 0.0), axis=1, keepdims=True
@@ -421,38 +445,60 @@
 
 
 def return_kernel(mine, theirs, out):
-    n_out, n = out.shape[0], mine.shape[0]
+    n_out, main = out.shape
+    n, width = mine.shape
+    tail = width - main
     row = rows_of((n_out, n))
     column = lanes_of((n_out, n))
     slot = row % GROUP
     base = (row // GROUP) * SLOTS
-    first = onehot((slot < SLOTS) & (column == base + slot))
-    second = onehot(
-        (slot >= SLOTS) & (slot < 2 * SLOTS) & (column == base + slot - SLOTS)
-    )
-    out[...] = (dot(first, mine[...]) + dot(second, theirs[...])).astype(BF)
+    own = onehot((slot < SLOTS) & (column == base + slot))
+    other = onehot((slot >= SLOTS) & (slot < 2 * SLOTS) & (column == base + slot - SLOTS))
+    value = dot(own, mine[:, :main]) + dot(other, theirs[:, :main])
+    out[...] = value.astype(BF)
+    for p in range(SLOTS):
+        own = onehot((slot == 2 * SLOTS) & (column == base + p))
+        other = onehot((slot == 2 * SLOTS + 1) & (column == base + p))
+        span = slice(p * tail, (p + 1) * tail)
+        rest = dot(own, mine[:, main:]) + dot(other, theirs[:, main:])
+        out[:, span] = (value[:, span] + rest).astype(BF)
 
 
 def combine_kernel(where, ids, logits, arrived, mixed, input_grad):
-    n_in = arrived.shape[0]
-    n_rows = mixed.shape[0]
+    n_in, main = arrived.shape
+    n_rows, width = mixed.shape
+    tail = width - main
     core = where[2]
-    shift = core * SLOTS
     first, second = gates(logits[...])
     row = rows_of((n_rows, n_in))
     lane = lanes_of((n_rows, n_in))
-    zero = jnp.zeros((n_rows, n_in), F32)
-    picks = [[zero, zero], [zero, zero]]
-    for t, k, expert, position in codes_of(ids):
-        base = expert * GROUP + position
-        picks[0][k] = jnp.where((row == t) & (lane == base + shift), 1.0, picks[0][k])
-        picks[1][k] = jnp.where(
-            (row == t) & (lane == base + SLOTS - shift), 1.0, picks[1][k]
+    data = arrived[...]
+    codes = codes_of(ids)
+
+    def picked(kind, k):
+        zero = jnp.zeros((n_rows, n_in), F32)
+        head, tails = zero, [zero] * SLOTS
+        for t, top, expert, position in codes:
+            if top != k:
+                continue
+            base = expert * GROUP
+            head = jnp.where(
+                (row == t) & (lane == base + kind * SLOTS + position), 1.0, head
+            )
+            here = (row == t) & (lane == base + 2 * SLOTS + kind)
+            for p in range(SLOTS):
+                tails[p] = jnp.where(here & (position == p), 1.0, tails[p])
+        rest = sum(
+            dot(tails[p].astype(BF), data[:, p * tail : (p + 1) * tail]) for p in range(SLOTS)
         )
-    data = arrived[...]
-    value = [[dot(p.astype(BF), data) for p in pair] for pair in picks]
-    mixed[...] = (first * value[0][0] + second * value[0][1]).astype(BF)
-    input_grad[...] = (value[1][0] + value[1][1]).astype(BF)
+        return dot(head.astype(BF), data[:, :main]), rest
+
+    spans = (slice(0, main), slice(main, width))
+    for out, kind, one, two in (
+        (mixed, core, first, second), (input_grad, 1 - core, 1.0, 1.0)
+    ):
+        for span, left, right in zip(spans, picked(kind, 0), picked(kind, 1)):
+            out[:, span] = (one * left + two * right).astype(BF)
 
 
 def shape(dims, dtype=BF):
@@ -530,13 +576,14 @@
         )(*[far_off(v) if plain else v for v in inputs[: scalars + plain]], *[near_by(v) for v in inputs[scalars + plain :]])
 
     ids, logits = expert_ids.T, router_logits.T
+    main = width * 2 * SLOTS // GROUP
     sent = call(
-        dispatch_kernel, held((n_experts * GROUP, width)),
+        dispatch_kernel, held((n_experts * GROUP, main + LANES)),
         ids, tenant_ids, logits, tokens, out_grad, scalars=2, plain=3,
     )
     arrived = lax.all_to_all(
-        sent.reshape(n_experts, GROUP, width), "expert", 0, 0, tiled=True
-    ).reshape(n_experts * GROUP, width)
+        sent.reshape(n_experts, GROUP, main + LANES), "expert", 0, 0, tiled=True
+    ).reshape(n_experts * GROUP, main + LANES)
 
     def loaded(kernel, out, *inputs, scalars=0, near=0):
         last = len(inputs) - near
@@ -644,10 +691,10 @@
         where, lines[0], *near, token_part, input_down_maps, output_up_map, scalars=1,
     )
     other = swapped(send)
-    back = call(return_kernel, held((n_experts * GROUP, width)), keep, other)
+    back = call(return_kernel, held((n_experts * GROUP, main)), keep, other)
     back = lax.all_to_all(
-        back.reshape(n_experts, GROUP, width), "expert", 0, 0, tiled=True
-    ).reshape(n_experts * GROUP, width)
+        back.reshape(n_experts, GROUP, main), "expert", 0, 0, tiled=True
+    ).reshape(n_experts * GROUP, main)
     input_down_gradient, output_up_gradient = call(
         adapter_grad_kernel,
         [shape((1, width, 2 * columns), F32), shape((1, columns, width), F32)],

time: 121 us -> 119 us (0.983)
  waiting for transfers between devices: 43.6 us -> 41.5 us
    all_to_all x2, waiting for transfers between devices: 14.9 us -> 12.8 us  [the longest x1 6.89 us: per_device(): lax.all_to_all(sent.reshape(n_experts, GROUP, main + LANES), 'expert', 0,...]
where the time goes in v1:
time: 119 us
  starting transfers between devices  47.2 us (40%)
  waiting for transfers between devices  41.5 us (35%)
  Pallas kernels  29 us (24%)
    ppermute x15, waiting for transfers between devices, turned(): return lax.ppermute(value, plane, turn(distance, stage))  25.5 us
    pallas_call x20, Pallas kernels, call(): pl.pallas_call(kernel, out_shape=out, in_specs=[smem()] * scalars + [vmem...  23.5 us
    ppermute x14, starting transfers between devices, swapped(): return lax.ppermute(value, 'dp', [(i, i ^ 1) for i in range(n_data)])  17.4 us
    ppermute x15, starting transfers between devices, turned(): return lax.ppermute(value, plane, turn(distance, stage))  17.4 us
    all_to_all x1, starting transfers between devices, per_device(): lax.all_to_all(sent.reshape(n_experts, GROUP, main + LANES), 'expert', 0,...  9 us
    all_to_all x1, waiting for transfers between devices, per_device(): lax.all_to_all(sent.reshape(n_experts, GROUP, main + LANES), 'expert', 0,...  6.89 us
    all_to_all x1, waiting for transfers between devices, per_device(): lax.all_to_all(back.reshape(n_experts, GROUP, main), 'expert', 0, 0, tile...  5.92 us
    pallas_call x2, Pallas kernels, loaded(): pl.pallas_call(kernel, out_shape=out, in_specs=[smem()] * scalars + [anyw...  5.54 us
  transfers between devices with their start and end apart: 31, of which 14 were waited for; matrix products, arithmetic and copies ran while one was open for 0% of the time, Pallas kernels for 13%

profile of v1, /device:TPU:1, one launch (start us, length us, event | category | flops | bytes accessed | tf_op | source)
XLA Modules:
  0.0 118.7 jit_solution(3955258590066704267)
XLA Ops:
  0.6 2.4 %shard_map.163 = bf16[64,1280]{1,0:T(8,128)(2,1)} custom-call(s32[2,8]{1,0:T(2,128)} %bitcast.11, s32[8]{0:T(128)} %tenants.1, f32[2,8]{1,0:T(2,128)} %bitcast.13, bf16[8,1536]{1,0:T(8,128)(2,1)} %tokens.1, bf16[8,1536]{1,0:T(8,128)(2,1)} %grads.1), custom_call_target="tpu_custom_call" | custom-call | tf_op jit(solution)/shard_map/pallas_call | solution.py:569
  3.0 9.0 %all-to-all-start = ((bf16[8,8,1280]{2,1,0:T(8,128)(2,1)}), bf16[8,8,1280]{2,1,0:T(8,128)(2,1)S(1)}, u32[]{:S(2)}, u32[]{:S(2)}) async-start(bf16[8,8,1280]{2,1,0:T(8,128)(2,1)} %bitcast.5), calls=%async_computation | async-start | bytes 327680 | tf_op jit(solution)/shard_map/all_to_all | solution.py:584
  12.0 1.2 %shard_map.164 = (bf16[1,1536,256]{2,1,0:T(8,128)(2,1)S(1)}, bf16[1,128,1536]{2,1,0:T(8,128)(2,1)S(1)}) custom-call(bf16[1,1536,256]{2,1,0:T(8,128)(2,1)} %down_maps.3, bf16[1,128,1536]{2,1,0:T(8,128)(2,1)} %up_map.3), custom_call_target="tpu_custom_call" | custom-call | tf_op jit(solution)/shard_map/pallas_call | solution.py:590
  13.4 6.9 %all-to-all-done = bf16[8,8,1280]{2,1,0:T(8,128)(2,1)S(1)} async-done(((bf16[8,8,1280]{2,1,0:T(8,128)(2,1)}), bf16[8,8,1280]{2,1,0:T(8,128)(2,1)S(1)}, u32[]{:S(2)}, u32[]{:S(2)}) %all-to-all-start) | async-done | bytes 163872 | tf_op jit(solution)/shard_map/all_to_all | solution.py:584
  21.5 2.6 %collective-permute-start = (bf16[24,1664]{1,0:T(8,128)(2,1)S(1)}, bf16[24,1664]{1,0:T(8,128)(2,1)S(1)}, u32[]{:S(2)}, u32[]{:S(2)}) collective-permute-start(bf16[24,1664]{1,0:T(8,128)(2,1)S(1)} %get-tuple-element.61), channel_id=1, source_target_pairs={{0,32},{32,0},{64,96},{96,64},{128,160},{160,128},{192,224},{224,1... | collective-permute-start | bytes 239624 | tf_op jit(solution)/shard_map/ppermute | solution.py:565
  25.5 1.4 %collective-permute-start.1 = (bf16[48,1664]{1,0:T(8,128)(2,1)S(1)}, bf16[48,1664]{1,0:T(8,128)(2,1)S(1)}, u32[]{:S(2)}, u32[]{:S(2)}) collective-permute-start(bf16[48,1664]{1,0:T(8,128)(2,1)S(1)} %shard_map.166.first._), channel_id=1, source_target_pairs={{0,1},{1,2},{2,3},{3,0},{32,96},{33,97},{34,98},{35,99},{64,65},{6... | collective-permute-start | bytes 479240 | tf_op jit(solution)/shard_map/ppermute | solution.py:562
  26.9 1.5 %collective-permute-start.3 = (bf16[48,1664]{1,0:T(8,128)(2,1)S(1)}, bf16[48,1664]{1,0:T(8,128)(2,1)S(1)}, u32[]{:S(2)}, u32[]{:S(2)}) collective-permute-start(bf16[48,1664]{1,0:T(8,128)(2,1)S(1)} %shard_map.166.first._), channel_id=1, source_target_pairs={{0,3},{1,0},{2,1},{3,2},{32,224},{33,225},{34,226},{35,227},{64,67... | collective-permute-start | bytes 479240 | tf_op jit(solution)/shard_map/ppermute | solution.py:562
  28.4 1.6 %collective-permute-start.2 = (bf16[48,1664]{1,0:T(8,128)(2,1)S(1)}, bf16[48,1664]{1,0:T(8,128)(2,1)S(1)}, u32[]{:S(2)}, u32[]{:S(2)}) collective-permute-start(bf16[48,1664]{1,0:T(8,128)(2,1)S(1)} %shard_map.166.first._), channel_id=1, source_target_pairs={{0,2},{1,3},{2,0},{3,1},{32,160},{33,161},{34,162},{35,163},{64,66... | collective-permute-start | bytes 479240 | tf_op jit(solution)/shard_map/ppermute | solution.py:562
  30.0 4.3 %shard_map.168 = (bf16[6144,256]{1,0:T(8,128)(2,1)S(1)}, bf16[6144,256]{1,0:T(8,128)(2,1)S(1)}, bf16[4,256,1536]{2,1,0:T(8,128)(2,1)S(1)}) custom-call(s32[3]{0:T(128)S(1)} %pad_add_fusion.where, bf16[1,6144,256]{2,1,0:T(8,128)(2,1)} %gate_w.1, bf16[1,6144,256]{2,1,0:T(8,128)(2,1)} %up_w.1, bf16[1,256,6144]{2,1,0:T(8,128)(2,1)} %down_w.1, ...), custom_call_target="tpu_custom_call" | custom-call | tf_op jit(solution)/shard_map/pallas_call | solution.py:590
  34.3 1.3 %collective-permute-start.4 = (bf16[2,48,1664]{2,1,0:T(8,128)(2,1)S(1)}, bf16[2,48,1664]{2,1,0:T(8,128)(2,1)S(1)}, u32[]{:S(2)}, u32[]{:S(2)}) collective-permute-start(bf16[2,48,1664]{2,1,0:T(8,128)(2,1)S(1)} %shard_map.167.refs_0_), channel_id=1, source_target_pairs={{0,64},{1,65},{2,66},{3,67},{32,33},{33,34},{34,35},{35,32},{64,12... | collective-permute-start | bytes 958472 | tf_op jit(solution)/shard_map/ppermute | solution.py:562
  35.6 1.5 %collective-permute-start.5 = (bf16[2,48,1664]{2,1,0:T(8,128)(2,1)S(1)}, bf16[2,48,1664]{2,1,0:T(8,128)(2,1)S(1)}, u32[]{:S(2)}, u32[]{:S(2)}) collective-permute-start(bf16[2,48,1664]{2,1,0:T(8,128)(2,1)S(1)} %shard_map.169.refs_1_), channel_id=1, source_target_pairs={{0,192},{1,193},{2,194},{3,195},{32,35},{33,32},{34,33},{35,34},{6... | collective-permute-start | bytes 958472 | tf_op jit(solution)/shard_map/ppermute | solution.py:562
  37.2 1.3 %collective-permute-start.7 = (bf16[2,48,1664]{2,1,0:T(8,128)(2,1)S(1)}, bf16[2,48,1664]{2,1,0:T(8,128)(2,1)S(1)}, u32[]{:S(2)}, u32[]{:S(2)}) collective-permute-start(bf16[2,48,1664]{2,1,0:T(8,128)(2,1)S(1)} %shard_map.167.refs_0_), channel_id=1, source_target_pairs={{0,192},{1,193},{2,194},{3,195},{32,35},{33,32},{34,33},{35,34},{6... | collective-permute-start | bytes 958472 | tf_op jit(solution)/shard_map/ppermute | solution.py:562
  38.7 2.5 %collective-permute-start.10 = (bf16[2,48,1664]{2,1,0:T(8,128)(2,1)S(1)}, bf16[2,48,1664]{2,1,0:T(8,128)(2,1)S(1)}, u32[]{:S(2)}, u32[]{:S(2)}) collective-permute-start(bf16[2,48,1664]{2,1,0:T(8,128)(2,1)S(1)} %shard_map.167.refs_0_), channel_id=1, source_target_pairs={{0,32},{32,0},{64,96},{96,64},{128,160},{160,128},{192,224},{224,1... | collective-permute-start | bytes 958472 | tf_op jit(solution)/shard_map/ppermute | solution.py:565
  41.7 1.9 %collective-permute-start.11 = (bf16[2,48,1664]{2,1,0:T(8,128)(2,1)S(1)}, bf16[2,48,1664]{2,1,0:T(8,128)(2,1)S(1)}, u32[]{:S(2)}, u32[]{:S(2)}) collective-permute-start(bf16[2,48,1664]{2,1,0:T(8,128)(2,1)S(1)} %shard_map.169.refs_1_), channel_id=1, source_target_pairs={{0,32},{32,0},{64,96},{96,64},{128,160},{160,128},{192,224},{224,1... | collective-permute-start | bytes 958472 | tf_op jit(solution)/shard_map/ppermute | solution.py:565
  46.5 1.5 %collective-permute-start.9 = (bf16[2,48,1664]{2,1,0:T(8,128)(2,1)S(1)}, bf16[2,48,1664]{2,1,0:T(8,128)(2,1)S(1)}, u32[]{:S(2)}, u32[]{:S(2)}) collective-permute-start(bf16[2,48,1664]{2,1,0:T(8,128)(2,1)S(1)} %collective-permute-done.5.refs_7_), channel_id=1, source_target_pairs={{0,192},{1,193},{2,194},{3,195},{32,35},{33,32},{34,33},{35,34},{6... | collective-permute-start | bytes 958472 | tf_op jit(solution)/shard_map/ppermute | solution.py:562
  48.0 2.5 %shard_map.170 = (bf16[4,512,1536]{2,1,0:T(8,128)(2,1)S(1)}, bf16[6144,256]{1,0:T(8,128)(2,1)S(1)}) custom-call(bf16[6144,256]{1,0:T(8,128)(2,1)S(1)} %get-tuple-element.66.gate_v.refs_16_, bf16[6144,256]{1,0:T(8,128)(2,1)S(1)} %get-tuple-element.67.up_v.refs_17_, bf16[4,256,1536]{2,1,0:T(8,128)(2,1)S(1)} %get-tuple-element.68.rest_0_.down_v.refs_18_), custom_call_target="tpu_custom_call" | custom-call | tf_op jit(solution)/shard_map/pallas_call | solution.py:569
  50.5 2.9 %collective-permute-start.17 = (bf16[2,48,1664]{2,1,0:T(8,128)(2,1)S(1)}, bf16[2,48,1664]{2,1,0:T(8,128)(2,1)S(1)}, u32[]{:S(2)}, u32[]{:S(2)}) collective-permute-start(bf16[2,48,1664]{2,1,0:T(8,128)(2,1)S(1)} %collective-permute-done.5.refs_7_), channel_id=1, source_target_pairs={{0,32},{32,0},{64,96},{96,64},{128,160},{160,128},{192,224},{224,1... | collective-permute-start | bytes 958472 | tf_op jit(solution)/shard_map/ppermute | solution.py:565
  53.9 1.9 %collective-permute-start.14 = (bf16[2,48,1664]{2,1,0:T(8,128)(2,1)S(1)}, bf16[2,48,1664]{2,1,0:T(8,128)(2,1)S(1)}, u32[]{:S(2)}, u32[]{:S(2)}) collective-permute-start(bf16[2,48,1664]{2,1,0:T(8,128)(2,1)S(1)} %collective-permute-done.8.refs_4_), channel_id=1, source_target_pairs={{0,32},{32,0},{64,96},{96,64},{128,160},{160,128},{192,224},{224,1... | collective-permute-start | bytes 958472 | tf_op jit(solution)/shard_map/ppermute | solution.py:565
  57.4 4.3 %shard_map.171 = (bf16[4,48,1536]{2,1,0:T(8,128)(2,1)S(1)}, bf16[4,48,1536]{2,1,0:T(8,128)(2,1)S(1)}, bf16[4,48,1536]{2,1,0:T(8,128)(2,1)S(1)}, bf16[4,48,1536]{...) custom-call(s32[3]{0:T(128)S(1)} %pad_add_fusion.where, ...), custom_call_target="tpu_custom_call" | custom-call | tf_op jit(solution)/shard_map/pallas_call | solution.py:569
  68.2 1.3 %collective-permute-start.20 = (bf16[4,48,1664]{2,1,0:T(8,128)(2,1)S(1)}, bf16[4,48,1664]{2,1,0:T(8,128)(2,1)S(1)}, u32[]{:S(2)}, u32[]{:S(2)}) collective-permute-start(bf16[4,48,1664]{2,1,0:T(8,128)(2,1)S(1)} %shard_map.174), channel_id=1, source_target_pairs={{0,192},{1,193},{2,194},{3,195},{32,35},{33,32},{34,33},{35,34},{6... | collective-permute-start | bytes 1916936 | tf_op jit(solution)/shard_map/ppermute | solution.py:562
  71.4 6.4 %collective-permute-done.20.near1 = bf16[4,48,1664]{2,1,0:T(8,128)(2,1)S(1)} collective-permute-done((bf16[4,48,1664]{2,1,0:T(8,128)(2,1)S(1)}, bf16[4,48,1664]{2,1,0:T(8,128)(2,1)S(1)}, u32[]{:S(2)}, u32[]{:S(2)}) %collective-permute-start.20) | collective-permute-done | bytes 639008 | tf_op jit(solution)/shard_map/ppermute | solution.py:562
  77.8 3.2 %collective-permute-done.22.near2 = bf16[4,48,1664]{2,1,0:T(8,128)(2,1)S(1)} collective-permute-done((bf16[4,48,1664]{2,1,0:T(8,128)(2,1)S(1)}, bf16[4,48,1664]{2,1,0:T(8,128)(2,1)S(1)}, u32[]{:S(2)}, u32[]{:S(2)}) %collective-permute-start.22) | collective-permute-done | bytes 639008 | tf_op jit(solution)/shard_map/ppermute | solution.py:562
  81.0 6.8 %collective-permute-done.24.near3 = bf16[4,48,1664]{2,1,0:T(8,128)(2,1)S(1)} collective-permute-done((bf16[4,48,1664]{2,1,0:T(8,128)(2,1)S(1)}, bf16[4,48,1664]{2,1,0:T(8,128)(2,1)S(1)}, u32[]{:S(2)}, u32[]{:S(2)}) %collective-permute-start.24) | collective-permute-done | bytes 639008 | tf_op jit(solution)/shard_map/ppermute | solution.py:562
  88.4 2.3 %collective-permute-start.25 = (bf16[48,2048]{1,0:T(8,128)(2,1)S(1)}, bf16[48,2048]{1,0:T(8,128)(2,1)S(1)}, u32[]{:S(2)}, u32[]{:S(2)}) collective-permute-start(bf16[48,2048]{1,0:T(8,128)(2,1)S(1)} %get-tuple-element.91), channel_id=1, source_target_pairs={{0,3},{1,0},{2,1},{3,2},{32,224},{33,225},{34,226},{35,227},{64,67... | collective-permute-start | bytes 589832 | tf_op jit(solution)/shard_map/ppermute | solution.py:562
  91.8 3.6 %collective-permute-done.25.near1 = bf16[48,2048]{1,0:T(8,128)(2,1)S(1)} collective-permute-done((bf16[48,2048]{1,0:T(8,128)(2,1)S(1)}, bf16[48,2048]{1,0:T(8,128)(2,1)S(1)}, u32[]{:S(2)}, u32[]{:S(2)}) %collective-permute-start.25) | collective-permute-done | bytes 196640 | tf_op jit(solution)/shard_map/ppermute | solution.py:562
  95.4 1.4 %collective-permute-done.26.near2 = bf16[48,2048]{1,0:T(8,128)(2,1)S(1)} collective-permute-done((bf16[48,2048]{1,0:T(8,128)(2,1)S(1)}, bf16[48,2048]{1,0:T(8,128)(2,1)S(1)}, u32[]{:S(2)}, u32[]{:S(2)}) %collective-permute-start.26) | collective-permute-done | bytes 196640 | tf_op jit(solution)/shard_map/ppermute | solution.py:562
  96.8 2.3 %collective-permute-done.27.near3 = bf16[48,2048]{1,0:T(8,128)(2,1)S(1)} collective-permute-done((bf16[48,2048]{1,0:T(8,128)(2,1)S(1)}, bf16[48,2048]{1,0:T(8,128)(2,1)S(1)}, u32[]{:S(2)}, u32[]{:S(2)}) %collective-permute-start.27) | collective-permute-done | bytes 196640 | tf_op jit(solution)/shard_map/ppermute | solution.py:562
  100.3 2.9 %collective-permute-start.28 = (bf16[24,1536]{1,0:T(8,128)(2,1)S(1)}, bf16[24,1536]{1,0:T(8,128)(2,1)S(1)}, u32[]{:S(2)}, u32[]{:S(2)}) collective-permute-start(bf16[24,1536]{1,0:T(8,128)(2,1)S(1)} %get-tuple-element.96), channel_id=1, source_target_pairs={{0,32},{32,0},{64,96},{96,64},{128,160},{160,128},{192,224},{224,1... | collective-permute-start | bytes 221192 | tf_op jit(solution)/shard_map/ppermute | solution.py:565
  105.1 3.4 %all-to-all-start.1 = ((bf16[8,8,1152]{2,1,0:T(8,128)(2,1)}), bf16[8,8,1152]{2,1,0:T(8,128)(2,1)S(1)}, u32[]{:S(2)}, u32[]{:S(2)}) async-start(bf16[8,8,1152]{2,1,0:T(8,128)(2,1)} %bitcast.7), calls=%async_computation.1 | async-start | bytes 294912 | tf_op jit(solution)/shard_map/all_to_all | solution.py:695
  109.5 1.7 %shard_map.183 = (f32[1,1536,256]{2,1,0:T(8,128)}, f32[1,128,1536]{2,1,0:T(8,128)}) custom-call(bf16[4,48,1664]{2,1,0:T(8,128)(2,1)S(1)} %get-tuple-element.94.token_part, bf16[4,48,1664]{2,1,0:T(8,128)(2,1)S(1)} %get-tuple-element.99.grad_part, bf16[4,48,128]{2,1,0:T(8,128)(2,1)S(1)} %get-tuple-element.100.down_rows, ...), custom_call_target="tpu_custom_call" | custom-call | tf_op jit(solution)/shard_map/pallas_call | solution.py:569
  111.2 5.9 %all-to-all-done.1 = bf16[8,8,1152]{2,1,0:T(8,128)(2,1)S(1)} async-done(((bf16[8,8,1152]{2,1,0:T(8,128)(2,1)}), bf16[8,8,1152]{2,1,0:T(8,128)(2,1)S(1)}, u32[]{:S(2)}, u32[]{:S(2)}) %all-to-all-start.1) | async-done | bytes 147488 | tf_op jit(solution)/shard_map/all_to_all | solution.py:695
  117.1 1.6 %shard_map.182 = (bf16[8,1536]{1,0:T(8,128)(2,1)}, bf16[8,1536]{1,0:T(8,128)(2,1)}) custom-call(s32[3]{0:T(128)S(1)} %pad_add_fusion.where, s32[2,8]{1,0:T(2,128)S(1)} %bitcast.12, f32[2,8]{1,0:T(2,128)S(1)} %bitcast.14, bf16[64,1152]{1,0:T(8,128)(2,1)S(1)} %bitcast.10), custom_call_target="tpu_custom_call" | custom-call | tf_op jit(solution)/shard_map/pallas_call | solution.py:569
  (65 shorter events, 22.9 us)
Async XLA Ops:
  3.0 17.2 %all-to-all-start = ((bf16[8,8,1280]{2,1,0:T(8,128)(2,1)}), bf16[8,8,1280]{2,1,0:T(8,128)(2,1)S(1)}, u32[]{:S(2)}, u32[]{:S(2)}) async-start(bf16[8,8,1280]{2,1,0:T(8,128)(2,1)} %bitcast.5), calls=%async_computation | async-start | bytes 327680 | tf_op jit(solution)/shard_map/all_to_all | solution.py:584
  21.5 3.5 %collective-permute-start = (bf16[24,1664]{1,0:T(8,128)(2,1)S(1)}, bf16[24,1664]{1,0:T(8,128)(2,1)S(1)}, u32[]{:S(2)}, u32[]{:S(2)}) collective-permute-start(bf16[24,1664]{1,0:T(8,128)(2,1)S(1)} %get-tuple-element.61), channel_id=1, source_target_pairs={{0,32},{32,0},{64,96},{96,64},{128,160},{160,128},{192,224},{224,1... | collective-permute-start | bytes 239624 | tf_op jit(solution)/shard_map/ppermute | solution.py:565
  25.5 8.8 %collective-permute-start.1 = (bf16[48,1664]{1,0:T(8,128)(2,1)S(1)}, bf16[48,1664]{1,0:T(8,128)(2,1)S(1)}, u32[]{:S(2)}, u32[]{:S(2)}) collective-permute-start(bf16[48,1664]{1,0:T(8,128)(2,1)S(1)} %shard_map.166.first._), channel_id=1, source_target_pairs={{0,1},{1,2},{2,3},{3,0},{32,96},{33,97},{34,98},{35,99},{64,65},{6... | collective-permute-start | bytes 479240 | tf_op jit(solution)/shard_map/ppermute | solution.py:562
  26.9 8.7 %collective-permute-start.3 = (bf16[48,1664]{1,0:T(8,128)(2,1)S(1)}, bf16[48,1664]{1,0:T(8,128)(2,1)S(1)}, u32[]{:S(2)}, u32[]{:S(2)}) collective-permute-start(bf16[48,1664]{1,0:T(8,128)(2,1)S(1)} %shard_map.166.first._), channel_id=1, source_target_pairs={{0,3},{1,0},{2,1},{3,2},{32,224},{33,225},{34,226},{35,227},{64,67... | collective-permute-start | bytes 479240 | tf_op jit(solution)/shard_map/ppermute | solution.py:562
  28.4 7.2 %collective-permute-start.2 = (bf16[48,1664]{1,0:T(8,128)(2,1)S(1)}, bf16[48,1664]{1,0:T(8,128)(2,1)S(1)}, u32[]{:S(2)}, u32[]{:S(2)}) collective-permute-start(bf16[48,1664]{1,0:T(8,128)(2,1)S(1)} %shard_map.166.first._), channel_id=1, source_target_pairs={{0,2},{1,3},{2,0},{3,1},{32,160},{33,161},{34,162},{35,163},{64,66... | collective-permute-start | bytes 479240 | tf_op jit(solution)/shard_map/ppermute | solution.py:562
  34.3 7.4 %collective-permute-start.4 = (bf16[2,48,1664]{2,1,0:T(8,128)(2,1)S(1)}, bf16[2,48,1664]{2,1,0:T(8,128)(2,1)S(1)}, u32[]{:S(2)}, u32[]{:S(2)}) collective-permute-start(bf16[2,48,1664]{2,1,0:T(8,128)(2,1)S(1)} %shard_map.167.refs_0_), channel_id=1, source_target_pairs={{0,64},{1,65},{2,66},{3,67},{32,33},{33,34},{34,35},{35,32},{64,12... | collective-permute-start | bytes 958472 | tf_op jit(solution)/shard_map/ppermute | solution.py:562
  35.6 8.0 %collective-permute-start.5 = (bf16[2,48,1664]{2,1,0:T(8,128)(2,1)S(1)}, bf16[2,48,1664]{2,1,0:T(8,128)(2,1)S(1)}, u32[]{:S(2)}, u32[]{:S(2)}) collective-permute-start(bf16[2,48,1664]{2,1,0:T(8,128)(2,1)S(1)} %shard_map.169.refs_1_), channel_id=1, source_target_pairs={{0,192},{1,193},{2,194},{3,195},{32,35},{33,32},{34,33},{35,34},{6... | collective-permute-start | bytes 958472 | tf_op jit(solution)/shard_map/ppermute | solution.py:562
  37.2 8.1 %collective-permute-start.7 = (bf16[2,48,1664]{2,1,0:T(8,128)(2,1)S(1)}, bf16[2,48,1664]{2,1,0:T(8,128)(2,1)S(1)}, u32[]{:S(2)}, u32[]{:S(2)}) collective-permute-start(bf16[2,48,1664]{2,1,0:T(8,128)(2,1)S(1)} %shard_map.167.refs_0_), channel_id=1, source_target_pairs={{0,192},{1,193},{2,194},{3,195},{32,35},{33,32},{34,33},{35,34},{6... | collective-permute-start | bytes 958472 | tf_op jit(solution)/shard_map/ppermute | solution.py:562
  38.5 8.0 %collective-permute-start.6 = (bf16[2,48,1664]{2,1,0:T(8,128)(2,1)S(1)}, bf16[2,48,1664]{2,1,0:T(8,128)(2,1)S(1)}, u32[]{:S(2)}, u32[]{:S(2)}) collective-permute-start(bf16[2,48,1664]{2,1,0:T(8,128)(2,1)S(1)} %shard_map.169.refs_1_), channel_id=1, source_target_pairs={{0,64},{1,65},{2,66},{3,67},{32,33},{33,34},{34,35},{35,32},{64,12... | collective-permute-start | bytes 958472 | tf_op jit(solution)/shard_map/ppermute | solution.py:562
  38.7 11.8 %collective-permute-start.10 = (bf16[2,48,1664]{2,1,0:T(8,128)(2,1)S(1)}, bf16[2,48,1664]{2,1,0:T(8,128)(2,1)S(1)}, u32[]{:S(2)}, u32[]{:S(2)}) collective-permute-start(bf16[2,48,1664]{2,1,0:T(8,128)(2,1)S(1)} %shard_map.167.refs_0_), channel_id=1, source_target_pairs={{0,32},{32,0},{64,96},{96,64},{128,160},{160,128},{192,224},{224,1... | collective-permute-start | bytes 958472 | tf_op jit(solution)/shard_map/ppermute | solution.py:565
  41.7 11.6 %collective-permute-start.11 = (bf16[2,48,1664]{2,1,0:T(8,128)(2,1)S(1)}, bf16[2,48,1664]{2,1,0:T(8,128)(2,1)S(1)}, u32[]{:S(2)}, u32[]{:S(2)}) collective-permute-start(bf16[2,48,1664]{2,1,0:T(8,128)(2,1)S(1)} %shard_map.169.refs_1_), channel_id=1, source_target_pairs={{0,32},{32,0},{64,96},{96,64},{128,160},{160,128},{192,224},{224,1... | collective-permute-start | bytes 958472 | tf_op jit(solution)/shard_map/ppermute | solution.py:565
  43.6 9.8 %collective-permute-start.12 = (bf16[2,48,1664]{2,1,0:T(8,128)(2,1)S(1)}, bf16[2,48,1664]{2,1,0:T(8,128)(2,1)S(1)}, u32[]{:S(2)}, u32[]{:S(2)}) collective-permute-start(bf16[2,48,1664]{2,1,0:T(8,128)(2,1)S(1)} %collective-permute-done.4.refs_2_), channel_id=1, source_target_pairs={{0,32},{32,0},{64,96},{96,64},{128,160},{160,128},{192,224},{224,1... | collective-permute-start | bytes 958472 | tf_op jit(solution)/shard_map/ppermute | solution.py:565
  45.3 8.6 %collective-permute-start.8 = (bf16[2,48,1664]{2,1,0:T(8,128)(2,1)S(1)}, bf16[2,48,1664]{2,1,0:T(8,128)(2,1)S(1)}, u32[]{:S(2)}, u32[]{:S(2)}) collective-permute-start(bf16[2,48,1664]{2,1,0:T(8,128)(2,1)S(1)} %collective-permute-done.4.refs_2_), channel_id=1, source_target_pairs={{0,64},{1,65},{2,66},{3,67},{32,33},{33,34},{34,35},{35,32},{64,12... | collective-permute-start | bytes 958472 | tf_op jit(solution)/shard_map/ppermute | solution.py:562
  46.5 9.2 %collective-permute-start.9 = (bf16[2,48,1664]{2,1,0:T(8,128)(2,1)S(1)}, bf16[2,48,1664]{2,1,0:T(8,128)(2,1)S(1)}, u32[]{:S(2)}, u32[]{:S(2)}) collective-permute-start(bf16[2,48,1664]{2,1,0:T(8,128)(2,1)S(1)} %collective-permute-done.5.refs_7_), channel_id=1, source_target_pairs={{0,192},{1,193},{2,194},{3,195},{32,35},{33,32},{34,33},{35,34},{6... | collective-permute-start | bytes 958472 | tf_op jit(solution)/shard_map/ppermute | solution.py:562
  50.5 5.6 %collective-permute-start.17 = (bf16[2,48,1664]{2,1,0:T(8,128)(2,1)S(1)}, bf16[2,48,1664]{2,1,0:T(8,128)(2,1)S(1)}, u32[]{:S(2)}, u32[]{:S(2)}) collective-permute-start(bf16[2,48,1664]{2,1,0:T(8,128)(2,1)S(1)} %collective-permute-done.5.refs_7_), channel_id=1, source_target_pairs={{0,32},{32,0},{64,96},{96,64},{128,160},{160,128},{192,224},{224,1... | collective-permute-start | bytes 958472 | tf_op jit(solution)/shard_map/ppermute | solution.py:565
  53.4 2.7 %collective-permute-start.13 = (bf16[2,48,1664]{2,1,0:T(8,128)(2,1)S(1)}, bf16[2,48,1664]{2,1,0:T(8,128)(2,1)S(1)}, u32[]{:S(2)}, u32[]{:S(2)}) collective-permute-start(bf16[2,48,1664]{2,1,0:T(8,128)(2,1)S(1)} %collective-permute-done.6.refs_3_), channel_id=1, source_target_pairs={{0,32},{32,0},{64,96},{96,64},{128,160},{160,128},{192,224},{224,1... | collective-permute-start | bytes 958472 | tf_op jit(solution)/shard_map/ppermute | solution.py:565
  53.5 2.6 %collective-permute-start.16 = (bf16[2,48,1664]{2,1,0:T(8,128)(2,1)S(1)}, bf16[2,48,1664]{2,1,0:T(8,128)(2,1)S(1)}, u32[]{:S(2)}, u32[]{:S(2)}) collective-permute-start(bf16[2,48,1664]{2,1,0:T(8,128)(2,1)S(1)} %collective-permute-done.7.refs_6_), channel_id=1, source_target_pairs={{0,32},{32,0},{64,96},{96,64},{128,160},{160,128},{192,224},{224,1... | collective-permute-start | bytes 958472 | tf_op jit(solution)/shard_map/ppermute | solution.py:565
  53.9 3.1 %collective-permute-start.14 = (bf16[2,48,1664]{2,1,0:T(8,128)(2,1)S(1)}, bf16[2,48,1664]{2,1,0:T(8,128)(2,1)S(1)}, u32[]{:S(2)}, u32[]{:S(2)}) collective-permute-start(bf16[2,48,1664]{2,1,0:T(8,128)(2,1)S(1)} %collective-permute-done.8.refs_4_), channel_id=1, source_target_pairs={{0,32},{32,0},{64,96},{96,64},{128,160},{160,128},{192,224},{224,1... | collective-permute-start | bytes 958472 | tf_op jit(solution)/shard_map/ppermute | solution.py:565
  55.7 1.7 %collective-permute-start.15 = (bf16[2,48,1664]{2,1,0:T(8,128)(2,1)S(1)}, bf16[2,48,1664]{2,1,0:T(8,128)(2,1)S(1)}, u32[]{:S(2)}, u32[]{:S(2)}) collective-permute-start(bf16[2,48,1664]{2,1,0:T(8,128)(2,1)S(1)} %collective-permute-done.9.refs_5_), channel_id=1, source_target_pairs={{0,32},{32,0},{64,96},{96,64},{128,160},{160,128},{192,224},{224,1... | collective-permute-start | bytes 958472 | tf_op jit(solution)/shard_map/ppermute | solution.py:565
  62.9 5.0 %collective-permute-start.19 = (bf16[4,48,1664]{2,1,0:T(8,128)(2,1)S(1)}, bf16[4,48,1664]{2,1,0:T(8,128)(2,1)S(1)}, u32[]{:S(2)}, u32[]{:S(2)}) collective-permute-start(bf16[4,48,1664]{2,1,0:T(8,128)(2,1)S(1)} %get-tuple-element.83), channel_id=1, source_target_pairs={{0,32},{32,0},{64,96},{96,64},{128,160},{160,128},{192,224},{224,1... | collective-permute-start | bytes 1916936 | tf_op jit(solution)/shard_map/ppermute | solution.py:565
  64.5 5.0 %collective-permute-start.21 = (bf16[4,48,1664]{2,1,0:T(8,128)(2,1)S(1)}, bf16[4,48,1664]{2,1,0:T(8,128)(2,1)S(1)}, u32[]{:S(2)}, u32[]{:S(2)}) collective-permute-start(bf16[4,48,1664]{2,1,0:T(8,128)(2,1)S(1)} %get-tuple-element.86), channel_id=1, source_target_pairs={{0,32},{32,0},{64,96},{96,64},{128,160},{160,128},{192,224},{224,1... | collective-permute-start | bytes 1916936 | tf_op jit(solution)/shard_map/ppermute | solution.py:565
  65.8 4.9 %collective-permute-start.23 = (bf16[4,48,1664]{2,1,0:T(8,128)(2,1)S(1)}, bf16[4,48,1664]{2,1,0:T(8,128)(2,1)S(1)}, u32[]{:S(2)}, u32[]{:S(2)}) collective-permute-start(bf16[4,48,1664]{2,1,0:T(8,128)(2,1)S(1)} %get-tuple-element.89), channel_id=1, source_target_pairs={{0,32},{32,0},{64,96},{96,64},{128,160},{160,128},{192,224},{224,1... | collective-permute-start | bytes 1916936 | tf_op jit(solution)/shard_map/ppermute | solution.py:565
  67.4 3.9 %collective-permute-start.18 = (bf16[4,48,1664]{2,1,0:T(8,128)(2,1)S(1)}, bf16[4,48,1664]{2,1,0:T(8,128)(2,1)S(1)}, u32[]{:S(2)}, u32[]{:S(2)}) collective-permute-start(bf16[4,48,1664]{2,1,0:T(8,128)(2,1)S(1)} %get-tuple-element.80), channel_id=1, source_target_pairs={{0,32},{32,0},{64,96},{96,64},{128,160},{160,128},{192,224},{224,1... | collective-permute-start | bytes 1916936 | tf_op jit(solution)/shard_map/ppermute | solution.py:565
  68.2 9.6 %collective-permute-start.20 = (bf16[4,48,1664]{2,1,0:T(8,128)(2,1)S(1)}, bf16[4,48,1664]{2,1,0:T(8,128)(2,1)S(1)}, u32[]{:S(2)}, u32[]{:S(2)}) collective-permute-start(bf16[4,48,1664]{2,1,0:T(8,128)(2,1)S(1)} %shard_map.174), channel_id=1, source_target_pairs={{0,192},{1,193},{2,194},{3,195},{32,35},{33,32},{34,33},{35,34},{6... | collective-permute-start | bytes 1916936 | tf_op jit(solution)/shard_map/ppermute | solution.py:562
  69.5 29.6 %copy-start.1 = (bf16[1,128,1536]{2,1,0:T(8,128)(2,1)S(1)}, bf16[1,128,1536]{2,1,0:T(8,128)(2,1)}, u32[]{:S(2)}) copy-start(bf16[1,128,1536]{2,1,0:T(8,128)(2,1)} %up_map.3) | copy-start | bytes 1179652
  69.8 11.2 %collective-permute-start.22 = (bf16[4,48,1664]{2,1,0:T(8,128)(2,1)S(1)}, bf16[4,48,1664]{2,1,0:T(8,128)(2,1)S(1)}, u32[]{:S(2)}, u32[]{:S(2)}) collective-permute-start(bf16[4,48,1664]{2,1,0:T(8,128)(2,1)S(1)} %shard_map.176), channel_id=1, source_target_pairs={{0,128},{1,129},{2,130},{3,131},{32,34},{33,35},{34,32},{35,33},{6... | collective-permute-start | bytes 1916936 | tf_op jit(solution)/shard_map/ppermute | solution.py:562
  71.1 16.7 %collective-permute-start.24 = (bf16[4,48,1664]{2,1,0:T(8,128)(2,1)S(1)}, bf16[4,48,1664]{2,1,0:T(8,128)(2,1)S(1)}, u32[]{:S(2)}, u32[]{:S(2)}) collective-permute-start(bf16[4,48,1664]{2,1,0:T(8,128)(2,1)S(1)} %shard_map.178), channel_id=1, source_target_pairs={{0,64},{1,65},{2,66},{3,67},{32,33},{33,34},{34,35},{35,32},{64,12... | collective-permute-start | bytes 1916936 | tf_op jit(solution)/shard_map/ppermute | solution.py:562
  88.4 7.0 %collective-permute-start.25 = (bf16[48,2048]{1,0:T(8,128)(2,1)S(1)}, bf16[48,2048]{1,0:T(8,128)(2,1)S(1)}, u32[]{:S(2)}, u32[]{:S(2)}) collective-permute-start(bf16[48,2048]{1,0:T(8,128)(2,1)S(1)} %get-tuple-element.91), channel_id=1, source_target_pairs={{0,3},{1,0},{2,1},{3,2},{32,224},{33,225},{34,226},{35,227},{64,67... | collective-permute-start | bytes 589832 | tf_op jit(solution)/shard_map/ppermute | solution.py:562
  90.7 6.1 %collective-permute-start.26 = (bf16[48,2048]{1,0:T(8,128)(2,1)S(1)}, bf16[48,2048]{1,0:T(8,128)(2,1)S(1)}, u32[]{:S(2)}, u32[]{:S(2)}) collective-permute-start(bf16[48,2048]{1,0:T(8,128)(2,1)S(1)} %get-tuple-element.92), channel_id=1, source_target_pairs={{0,2},{1,3},{2,0},{3,1},{32,160},{33,161},{34,162},{35,163},{64,66... | collective-permute-start | bytes 589832 | tf_op jit(solution)/shard_map/ppermute | solution.py:562
  91.0 8.1 %collective-permute-start.27 = (bf16[48,2048]{1,0:T(8,128)(2,1)S(1)}, bf16[48,2048]{1,0:T(8,128)(2,1)S(1)}, u32[]{:S(2)}, u32[]{:S(2)}) collective-permute-start(bf16[48,2048]{1,0:T(8,128)(2,1)S(1)} %get-tuple-element.93), channel_id=1, source_target_pairs={{0,1},{1,2},{2,3},{3,0},{32,96},{33,97},{34,98},{35,99},{64,65},{6... | collective-permute-start | bytes 589832 | tf_op jit(solution)/shard_map/ppermute | solution.py:562
  100.3 3.8 %collective-permute-start.28 = (bf16[24,1536]{1,0:T(8,128)(2,1)S(1)}, bf16[24,1536]{1,0:T(8,128)(2,1)S(1)}, u32[]{:S(2)}, u32[]{:S(2)}) collective-permute-start(bf16[24,1536]{1,0:T(8,128)(2,1)S(1)} %get-tuple-element.96), channel_id=1, source_target_pairs={{0,32},{32,0},{64,96},{96,64},{128,160},{160,128},{192,224},{224,1... | collective-permute-start | bytes 221192 | tf_op jit(solution)/shard_map/ppermute | solution.py:565
  105.1 12.0 %all-to-all-start.1 = ((bf16[8,8,1152]{2,1,0:T(8,128)(2,1)}), bf16[8,8,1152]{2,1,0:T(8,128)(2,1)S(1)}, u32[]{:S(2)}, u32[]{:S(2)}) async-start(bf16[8,8,1152]{2,1,0:T(8,128)(2,1)} %bitcast.7), calls=%async_computation.1 | async-start | bytes 294912 | tf_op jit(solution)/shard_map/all_to_all | solution.py:695
  (5 other events, 114.7 us)

commit v2 on v1

--- a/solution.py
+++ b/solution.py
@@ -194,8 +194,7 @@
         out[n:] = mine[...]
 
 
-def stack_kernel(first, second, *rest):
-    out = rest[-1]
+def stack_kernel(first, second, out):
     out[0] = first[...]
     out[1] = second[...]
 
@@ -619,7 +618,7 @@
         scalars=1, near=1,
     )
     crossed = [held((n, 2 * hidden, width)), held((n * width, hidden))]
-    line_b = call(stack_kernel, held((2, pair, wide)), *line[2:], weights[2])
+    line_b = call(stack_kernel, held((2, pair, wide)), *line[2:])
     line_a = call(stack_kernel, held((2, pair, wide)), *line[:2])
     near_a, far_b = turned(line_a, 1, 1), turned(line_b, n - 1, 1)
     near_b, far_a = turned(line_b, 1, 1), turned(line_a, n - 1, 1)

time: 119 us -> 119 us (level)
    ppermute x14, starting transfers between devices: 17.4 us -> 15.4 us  [swapped(): return lax.ppermute(value, 'dp', [(i, i ^ 1) for i in range(n_data)])]
    ppermute x15, starting transfers between devices: 17.4 us -> 19.1 us  [turned(): return lax.ppermute(value, plane, turn(distance, stage))]
where the time goes in v2:
time: 119 us
  starting transfers between devices  46.9 us (39%)
  waiting for transfers between devices  41.8 us (35%)
  Pallas kernels  29.1 us (24%)
    ppermute x15, waiting for transfers between devices, turned(): return lax.ppermute(value, plane, turn(distance, stage))  25.5 us
    pallas_call x20, Pallas kernels, call(): pl.pallas_call(kernel, out_shape=out, in_specs=[smem()] * scalars + [vmem...  23.5 us
    ppermute x15, starting transfers between devices, turned(): return lax.ppermute(value, plane, turn(distance, stage))  19.1 us
    ppermute x14, starting transfers between devices, swapped(): return lax.ppermute(value, 'dp', [(i, i ^ 1) for i in range(n_data)])  15.4 us
    all_to_all x1, starting transfers between devices, per_device(): lax.all_to_all(sent.reshape(n_experts, GROUP, main + LANES), 'expert', 0,...  9 us
    all_to_all x1, waiting for transfers between devices, per_device(): lax.all_to_all(sent.reshape(n_experts, GROUP, main + LANES), 'expert', 0,...  6.89 us
    all_to_all x1, waiting for transfers between devices, per_device(): lax.all_to_all(back.reshape(n_experts, GROUP, main), 'expert', 0, 0, tile...  5.91 us
    pallas_call x2, Pallas kernels, loaded(): pl.pallas_call(kernel, out_shape=out, in_specs=[smem()] * scalars + [anyw...  5.54 us
  transfers between devices with their start and end apart: 31, of which 14 were waited for; matrix products, arithmetic and copies ran while one was open for 0% of the time, Pallas kernels for 13%

profile of v2, /device:TPU:1, one launch (start us, length us, event | category | flops | bytes accessed | tf_op | source)
XLA Modules:
  0.0 118.7 jit_solution(13517191250355173411)
XLA Ops:
  0.6 2.4 %shard_map.163 = bf16[64,1280]{1,0:T(8,128)(2,1)} custom-call(s32[2,8]{1,0:T(2,128)} %bitcast.11, s32[8]{0:T(128)} %tenants.1, f32[2,8]{1,0:T(2,128)} %bitcast.13, bf16[8,1536]{1,0:T(8,128)(2,1)} %tokens.1, bf16[8,1536]{1,0:T(8,128)(2,1)} %grads.1), custom_call_target="tpu_custom_call" | custom-call | tf_op jit(solution)/shard_map/pallas_call | solution.py:568
  3.0 9.0 %all-to-all-start = ((bf16[8,8,1280]{2,1,0:T(8,128)(2,1)}), bf16[8,8,1280]{2,1,0:T(8,128)(2,1)S(1)}, u32[]{:S(2)}, u32[]{:S(2)}) async-start(bf16[8,8,1280]{2,1,0:T(8,128)(2,1)} %bitcast.5), calls=%async_computation | async-start | bytes 327680 | tf_op jit(solution)/shard_map/all_to_all | solution.py:583
  12.0 1.2 %shard_map.164 = (bf16[1,1536,256]{2,1,0:T(8,128)(2,1)S(1)}, bf16[1,128,1536]{2,1,0:T(8,128)(2,1)S(1)}) custom-call(bf16[1,1536,256]{2,1,0:T(8,128)(2,1)} %down_maps.3, bf16[1,128,1536]{2,1,0:T(8,128)(2,1)} %up_map.3), custom_call_target="tpu_custom_call" | custom-call | tf_op jit(solution)/shard_map/pallas_call | solution.py:589
  13.4 6.9 %all-to-all-done = bf16[8,8,1280]{2,1,0:T(8,128)(2,1)S(1)} async-done(((bf16[8,8,1280]{2,1,0:T(8,128)(2,1)}), bf16[8,8,1280]{2,1,0:T(8,128)(2,1)S(1)}, u32[]{:S(2)}, u32[]{:S(2)}) %all-to-all-start) | async-done | bytes 163872 | tf_op jit(solution)/shard_map/all_to_all | solution.py:583
  21.5 2.6 %collective-permute-start = (bf16[24,1664]{1,0:T(8,128)(2,1)S(1)}, bf16[24,1664]{1,0:T(8,128)(2,1)S(1)}, u32[]{:S(2)}, u32[]{:S(2)}) collective-permute-start(bf16[24,1664]{1,0:T(8,128)(2,1)S(1)} %get-tuple-element.61), channel_id=1, source_target_pairs={{0,32},{32,0},{64,96},{96,64},{128,160},{160,128},{192,224},{224,1... | collective-permute-start | bytes 239624 | tf_op jit(solution)/shard_map/ppermute | solution.py:564
  25.5 1.4 %collective-permute-start.1 = (bf16[48,1664]{1,0:T(8,128)(2,1)S(1)}, bf16[48,1664]{1,0:T(8,128)(2,1)S(1)}, u32[]{:S(2)}, u32[]{:S(2)}) collective-permute-start(bf16[48,1664]{1,0:T(8,128)(2,1)S(1)} %shard_map.166.first._), channel_id=1, source_target_pairs={{0,1},{1,2},{2,3},{3,0},{32,96},{33,97},{34,98},{35,99},{64,65},{6... | collective-permute-start | bytes 479240 | tf_op jit(solution)/shard_map/ppermute | solution.py:561
  26.9 1.5 %collective-permute-start.3 = (bf16[48,1664]{1,0:T(8,128)(2,1)S(1)}, bf16[48,1664]{1,0:T(8,128)(2,1)S(1)}, u32[]{:S(2)}, u32[]{:S(2)}) collective-permute-start(bf16[48,1664]{1,0:T(8,128)(2,1)S(1)} %shard_map.166.first._), channel_id=1, source_target_pairs={{0,3},{1,0},{2,1},{3,2},{32,224},{33,225},{34,226},{35,227},{64,67... | collective-permute-start | bytes 479240 | tf_op jit(solution)/shard_map/ppermute | solution.py:561
  28.4 1.6 %collective-permute-start.2 = (bf16[48,1664]{1,0:T(8,128)(2,1)S(1)}, bf16[48,1664]{1,0:T(8,128)(2,1)S(1)}, u32[]{:S(2)}, u32[]{:S(2)}) collective-permute-start(bf16[48,1664]{1,0:T(8,128)(2,1)S(1)} %shard_map.166.first._), channel_id=1, source_target_pairs={{0,2},{1,3},{2,0},{3,1},{32,160},{33,161},{34,162},{35,163},{64,66... | collective-permute-start | bytes 479240 | tf_op jit(solution)/shard_map/ppermute | solution.py:561
  30.0 1.3 %collective-permute-done.1.second = bf16[48,1664]{1,0:T(8,128)(2,1)S(1)} collective-permute-done((bf16[48,1664]{1,0:T(8,128)(2,1)S(1)}, bf16[48,1664]{1,0:T(8,128)(2,1)S(1)}, u32[]{:S(2)}, u32[]{:S(2)}) %collective-permute-start.1) | collective-permute-done | bytes 159776 | tf_op jit(solution)/shard_map/ppermute | solution.py:561
  32.3 2.0 %collective-permute-done.2.first = bf16[48,1664]{1,0:T(8,128)(2,1)S(1)} collective-permute-done((bf16[48,1664]{1,0:T(8,128)(2,1)S(1)}, bf16[48,1664]{1,0:T(8,128)(2,1)S(1)}, u32[]{:S(2)}, u32[]{:S(2)}) %collective-permute-start.2) | collective-permute-done | bytes 159776 | tf_op jit(solution)/shard_map/ppermute | solution.py:561
  34.4 2.6 %collective-permute-start.5 = (bf16[2,48,1664]{2,1,0:T(8,128)(2,1)S(1)}, bf16[2,48,1664]{2,1,0:T(8,128)(2,1)S(1)}, u32[]{:S(2)}, u32[]{:S(2)}) collective-permute-start(bf16[2,48,1664]{2,1,0:T(8,128)(2,1)S(1)} %shard_map.168.refs_1_), channel_id=1, source_target_pairs={{0,192},{1,193},{2,194},{3,195},{32,35},{33,32},{34,33},{35,34},{6... | collective-permute-start | bytes 958472 | tf_op jit(solution)/shard_map/ppermute | solution.py:561
  38.4 4.3 %shard_map.169 = (bf16[6144,256]{1,0:T(8,128)(2,1)S(1)}, bf16[6144,256]{1,0:T(8,128)(2,1)S(1)}, bf16[4,256,1536]{2,1,0:T(8,128)(2,1)S(1)}) custom-call(s32[3]{0:T(128)S(1)} %pad_add_fusion.where, bf16[1,6144,256]{2,1,0:T(8,128)(2,1)} %gate_w.1, bf16[1,6144,256]{2,1,0:T(8,128)(2,1)} %up_w.1, bf16[1,256,6144]{2,1,0:T(8,128)(2,1)} %down_w.1, ...), custom_call_target="tpu_custom_call" | custom-call | tf_op jit(solution)/shard_map/pallas_call | solution.py:589
  42.7 3.4 %collective-permute-start.10 = (bf16[2,48,1664]{2,1,0:T(8,128)(2,1)S(1)}, bf16[2,48,1664]{2,1,0:T(8,128)(2,1)S(1)}, u32[]{:S(2)}, u32[]{:S(2)}) collective-permute-start(bf16[2,48,1664]{2,1,0:T(8,128)(2,1)S(1)} %shard_map.167.refs_0_), channel_id=1, source_target_pairs={{0,32},{32,0},{64,96},{96,64},{128,160},{160,128},{192,224},{224,1... | collective-permute-start | bytes 958472 | tf_op jit(solution)/shard_map/ppermute | solution.py:564
  46.7 2.7 %collective-permute-start.9 = (bf16[2,48,1664]{2,1,0:T(8,128)(2,1)S(1)}, bf16[2,48,1664]{2,1,0:T(8,128)(2,1)S(1)}, u32[]{:S(2)}, u32[]{:S(2)}) collective-permute-start(bf16[2,48,1664]{2,1,0:T(8,128)(2,1)S(1)} %collective-permute-done.5.refs_7_), channel_id=1, source_target_pairs={{0,192},{1,193},{2,194},{3,195},{32,35},{33,32},{34,33},{35,34},{6... | collective-permute-start | bytes 958472 | tf_op jit(solution)/shard_map/ppermute | solution.py:561
  49.4 2.5 %shard_map.170 = (bf16[4,512,1536]{2,1,0:T(8,128)(2,1)S(1)}, bf16[6144,256]{1,0:T(8,128)(2,1)S(1)}) custom-call(bf16[6144,256]{1,0:T(8,128)(2,1)S(1)} %get-tuple-element.66.gate_v.refs_16_, bf16[6144,256]{1,0:T(8,128)(2,1)S(1)} %get-tuple-element.67.up_v.refs_17_, bf16[4,256,1536]{2,1,0:T(8,128)(2,1)S(1)} %get-tuple-element.68.down_v.refs_18_), custom_call_target="tpu_custom_call" | custom-call | tf_op jit(solution)/shard_map/pallas_call | solution.py:568
  51.9 2.1 %collective-permute-start.17 = (bf16[2,48,1664]{2,1,0:T(8,128)(2,1)S(1)}, bf16[2,48,1664]{2,1,0:T(8,128)(2,1)S(1)}, u32[]{:S(2)}, u32[]{:S(2)}) collective-permute-start(bf16[2,48,1664]{2,1,0:T(8,128)(2,1)S(1)} %collective-permute-done.5.refs_7_), channel_id=1, source_target_pairs={{0,32},{32,0},{64,96},{96,64},{128,160},{160,128},{192,224},{224,1... | collective-permute-start | bytes 958472 | tf_op jit(solution)/shard_map/ppermute | solution.py:564
  54.5 1.8 %collective-permute-start.14 = (bf16[2,48,1664]{2,1,0:T(8,128)(2,1)S(1)}, bf16[2,48,1664]{2,1,0:T(8,128)(2,1)S(1)}, u32[]{:S(2)}, u32[]{:S(2)}) collective-permute-start(bf16[2,48,1664]{2,1,0:T(8,128)(2,1)S(1)} %collective-permute-done.8.refs_4_), channel_id=1, source_target_pairs={{0,32},{32,0},{64,96},{96,64},{128,160},{160,128},{192,224},{224,1... | collective-permute-start | bytes 958472 | tf_op jit(solution)/shard_map/ppermute | solution.py:564
  58.0 4.3 %shard_map.171 = (bf16[4,48,1536]{2,1,0:T(8,128)(2,1)S(1)}, bf16[4,48,1536]{2,1,0:T(8,128)(2,1)S(1)}, bf16[4,48,1536]{2,1,0:T(8,128)(2,1)S(1)}, bf16[4,48,1536]{...) custom-call(s32[3]{0:T(128)S(1)} %pad_add_fusion.where, ...), custom_call_target="tpu_custom_call" | custom-call | tf_op jit(solution)/shard_map/pallas_call | solution.py:568
  69.7 2.0 %collective-permute-start.22 = (bf16[4,48,1664]{2,1,0:T(8,128)(2,1)S(1)}, bf16[4,48,1664]{2,1,0:T(8,128)(2,1)S(1)}, u32[]{:S(2)}, u32[]{:S(2)}) collective-permute-start(bf16[4,48,1664]{2,1,0:T(8,128)(2,1)S(1)} %shard_map.176), channel_id=1, source_target_pairs={{0,128},{1,129},{2,130},{3,131},{32,34},{33,35},{34,32},{35,33},{6... | collective-permute-start | bytes 1916936 | tf_op jit(solution)/shard_map/ppermute | solution.py:561
  72.9 5.4 %collective-permute-done.20.near1 = bf16[4,48,1664]{2,1,0:T(8,128)(2,1)S(1)} collective-permute-done((bf16[4,48,1664]{2,1,0:T(8,128)(2,1)S(1)}, bf16[4,48,1664]{2,1,0:T(8,128)(2,1)S(1)}, u32[]{:S(2)}, u32[]{:S(2)}) %collective-permute-start.20) | collective-permute-done | bytes 639008 | tf_op jit(solution)/shard_map/ppermute | solution.py:561
  78.4 2.6 %collective-permute-done.22.near2 = bf16[4,48,1664]{2,1,0:T(8,128)(2,1)S(1)} collective-permute-done((bf16[4,48,1664]{2,1,0:T(8,128)(2,1)S(1)}, bf16[4,48,1664]{2,1,0:T(8,128)(2,1)S(1)}, u32[]{:S(2)}, u32[]{:S(2)}) %collective-permute-start.22) | collective-permute-done | bytes 639008 | tf_op jit(solution)/shard_map/ppermute | solution.py:561
  80.9 6.8 %collective-permute-done.24.near3 = bf16[4,48,1664]{2,1,0:T(8,128)(2,1)S(1)} collective-permute-done((bf16[4,48,1664]{2,1,0:T(8,128)(2,1)S(1)}, bf16[4,48,1664]{2,1,0:T(8,128)(2,1)S(1)}, u32[]{:S(2)}, u32[]{:S(2)}) %collective-permute-start.24) | collective-permute-done | bytes 639008 | tf_op jit(solution)/shard_map/ppermute | solution.py:561
  88.4 2.3 %collective-permute-start.25 = (bf16[48,2048]{1,0:T(8,128)(2,1)S(1)}, bf16[48,2048]{1,0:T(8,128)(2,1)S(1)}, u32[]{:S(2)}, u32[]{:S(2)}) collective-permute-start(bf16[48,2048]{1,0:T(8,128)(2,1)S(1)} %get-tuple-element.91), channel_id=1, source_target_pairs={{0,3},{1,0},{2,1},{3,2},{32,224},{33,225},{34,226},{35,227},{64,67... | collective-permute-start | bytes 589832 | tf_op jit(solution)/shard_map/ppermute | solution.py:561
  91.8 3.6 %collective-permute-done.25.near1 = bf16[48,2048]{1,0:T(8,128)(2,1)S(1)} collective-permute-done((bf16[48,2048]{1,0:T(8,128)(2,1)S(1)}, bf16[48,2048]{1,0:T(8,128)(2,1)S(1)}, u32[]{:S(2)}, u32[]{:S(2)}) %collective-permute-start.25) | collective-permute-done | bytes 196640 | tf_op jit(solution)/shard_map/ppermute | solution.py:561
  95.4 1.4 %collective-permute-done.26.near2 = bf16[48,2048]{1,0:T(8,128)(2,1)S(1)} collective-permute-done((bf16[48,2048]{1,0:T(8,128)(2,1)S(1)}, bf16[48,2048]{1,0:T(8,128)(2,1)S(1)}, u32[]{:S(2)}, u32[]{:S(2)}) %collective-permute-start.26) | collective-permute-done | bytes 196640 | tf_op jit(solution)/shard_map/ppermute | solution.py:561
  96.8 2.3 %collective-permute-done.27.near3 = bf16[48,2048]{1,0:T(8,128)(2,1)S(1)} collective-permute-done((bf16[48,2048]{1,0:T(8,128)(2,1)S(1)}, bf16[48,2048]{1,0:T(8,128)(2,1)S(1)}, u32[]{:S(2)}, u32[]{:S(2)}) %collective-permute-start.27) | collective-permute-done | bytes 196640 | tf_op jit(solution)/shard_map/ppermute | solution.py:561
  99.1 1.2 %shard_map.180 = (bf16[24,1536]{1,0:T(8,128)(2,1)S(1)}, bf16[24,1536]{1,0:T(8,128)(2,1)S(1)}, bf16[4,48,128]{2,1,0:T(8,128)(2,1)S(1)}, bf16[4,48,256]{2,1,0:T(8,128)(2,1)S(1)}) custom-call(s32[3]{0:T(128)S(1)} %pad_add_fusion.where, bf16[48,2048]{1,0:T(8,128)(2,1)S(1)} %get-tuple-element.90.mine, bf16[48,2048]{1,0:T(8,128)(2,1)S(1)} %collective-permute-done.25.near1, ...), custom_call_target="tpu_custom_call" | custom-call | tf_op jit(solution)/shard_map/pallas_call | solution.py:568
  100.3 2.9 %collective-permute-start.28 = (bf16[24,1536]{1,0:T(8,128)(2,1)S(1)}, bf16[24,1536]{1,0:T(8,128)(2,1)S(1)}, u32[]{:S(2)}, u32[]{:S(2)}) collective-permute-start(bf16[24,1536]{1,0:T(8,128)(2,1)S(1)} %get-tuple-element.96), channel_id=1, source_target_pairs={{0,32},{32,0},{64,96},{96,64},{128,160},{160,128},{192,224},{224,1... | collective-permute-start | bytes 221192 | tf_op jit(solution)/shard_map/ppermute | solution.py:564
  105.1 3.4 %all-to-all-start.1 = ((bf16[8,8,1152]{2,1,0:T(8,128)(2,1)}), bf16[8,8,1152]{2,1,0:T(8,128)(2,1)S(1)}, u32[]{:S(2)}, u32[]{:S(2)}) async-start(bf16[8,8,1152]{2,1,0:T(8,128)(2,1)} %bitcast.7), calls=%async_computation.1 | async-start | bytes 294912 | tf_op jit(solution)/shard_map/all_to_all | solution.py:694
  109.5 1.7 %shard_map.183 = (f32[1,1536,256]{2,1,0:T(8,128)}, f32[1,128,1536]{2,1,0:T(8,128)}) custom-call(bf16[4,48,1664]{2,1,0:T(8,128)(2,1)S(1)} %get-tuple-element.94.token_part, bf16[4,48,1664]{2,1,0:T(8,128)(2,1)S(1)} %get-tuple-element.99.grad_part, bf16[4,48,128]{2,1,0:T(8,128)(2,1)S(1)} %get-tuple-element.100.down_rows, ...), custom_call_target="tpu_custom_call" | custom-call | tf_op jit(solution)/shard_map/pallas_call | solution.py:568
  111.2 5.9 %all-to-all-done.1 = bf16[8,8,1152]{2,1,0:T(8,128)(2,1)S(1)} async-done(((bf16[8,8,1152]{2,1,0:T(8,128)(2,1)}), bf16[8,8,1152]{2,1,0:T(8,128)(2,1)S(1)}, u32[]{:S(2)}, u32[]{:S(2)}) %all-to-all-start.1) | async-done | bytes 147488 | tf_op jit(solution)/shard_map/all_to_all | solution.py:694
  117.1 1.6 %shard_map.182 = (bf16[8,1536]{1,0:T(8,128)(2,1)}, bf16[8,1536]{1,0:T(8,128)(2,1)}) custom-call(s32[3]{0:T(128)S(1)} %pad_add_fusion.where, s32[2,8]{1,0:T(2,128)S(1)} %bitcast.12, f32[2,8]{1,0:T(2,128)S(1)} %bitcast.14, bf16[64,1152]{1,0:T(8,128)(2,1)S(1)} %bitcast.10), custom_call_target="tpu_custom_call" | custom-call | tf_op jit(solution)/shard_map/pallas_call | solution.py:568
  (65 shorter events, 21.2 us)
Async XLA Ops:
  3.0 17.2 %all-to-all-start = ((bf16[8,8,1280]{2,1,0:T(8,128)(2,1)}), bf16[8,8,1280]{2,1,0:T(8,128)(2,1)S(1)}, u32[]{:S(2)}, u32[]{:S(2)}) async-start(bf16[8,8,1280]{2,1,0:T(8,128)(2,1)} %bitcast.5), calls=%async_computation | async-start | bytes 327680 | tf_op jit(solution)/shard_map/all_to_all | solution.py:583
  21.5 3.5 %collective-permute-start = (bf16[24,1664]{1,0:T(8,128)(2,1)S(1)}, bf16[24,1664]{1,0:T(8,128)(2,1)S(1)}, u32[]{:S(2)}, u32[]{:S(2)}) collective-permute-start(bf16[24,1664]{1,0:T(8,128)(2,1)S(1)} %get-tuple-element.61), channel_id=1, source_target_pairs={{0,32},{32,0},{64,96},{96,64},{128,160},{160,128},{192,224},{224,1... | collective-permute-start | bytes 239624 | tf_op jit(solution)/shard_map/ppermute | solution.py:564
  25.5 5.8 %collective-permute-start.1 = (bf16[48,1664]{1,0:T(8,128)(2,1)S(1)}, bf16[48,1664]{1,0:T(8,128)(2,1)S(1)}, u32[]{:S(2)}, u32[]{:S(2)}) collective-permute-start(bf16[48,1664]{1,0:T(8,128)(2,1)S(1)} %shard_map.166.first._), channel_id=1, source_target_pairs={{0,1},{1,2},{2,3},{3,0},{32,96},{33,97},{34,98},{35,99},{64,65},{6... | collective-permute-start | bytes 479240 | tf_op jit(solution)/shard_map/ppermute | solution.py:561
  26.9 5.4 %collective-permute-start.3 = (bf16[48,1664]{1,0:T(8,128)(2,1)S(1)}, bf16[48,1664]{1,0:T(8,128)(2,1)S(1)}, u32[]{:S(2)}, u32[]{:S(2)}) collective-permute-start(bf16[48,1664]{1,0:T(8,128)(2,1)S(1)} %shard_map.166.first._), channel_id=1, source_target_pairs={{0,3},{1,0},{2,1},{3,2},{32,224},{33,225},{34,226},{35,227},{64,67... | collective-permute-start | bytes 479240 | tf_op jit(solution)/shard_map/ppermute | solution.py:561
  28.4 5.9 %collective-permute-start.2 = (bf16[48,1664]{1,0:T(8,128)(2,1)S(1)}, bf16[48,1664]{1,0:T(8,128)(2,1)S(1)}, u32[]{:S(2)}, u32[]{:S(2)}) collective-permute-start(bf16[48,1664]{1,0:T(8,128)(2,1)S(1)} %shard_map.166.first._), channel_id=1, source_target_pairs={{0,2},{1,3},{2,0},{3,1},{32,160},{33,161},{34,162},{35,163},{64,66... | collective-permute-start | bytes 479240 | tf_op jit(solution)/shard_map/ppermute | solution.py:561
  31.3 14.8 %collective-permute-start.4 = (bf16[2,48,1664]{2,1,0:T(8,128)(2,1)S(1)}, bf16[2,48,1664]{2,1,0:T(8,128)(2,1)S(1)}, u32[]{:S(2)}, u32[]{:S(2)}) collective-permute-start(bf16[2,48,1664]{2,1,0:T(8,128)(2,1)S(1)} %shard_map.167.refs_0_), channel_id=1, source_target_pairs={{0,64},{1,65},{2,66},{3,67},{32,33},{33,34},{34,35},{35,32},{64,12... | collective-permute-start | bytes 958472 | tf_op jit(solution)/shard_map/ppermute | solution.py:561
  34.4 11.9 %collective-permute-start.5 = (bf16[2,48,1664]{2,1,0:T(8,128)(2,1)S(1)}, bf16[2,48,1664]{2,1,0:T(8,128)(2,1)S(1)}, u32[]{:S(2)}, u32[]{:S(2)}) collective-permute-start(bf16[2,48,1664]{2,1,0:T(8,128)(2,1)S(1)} %shard_map.168.refs_1_), channel_id=1, source_target_pairs={{0,192},{1,193},{2,194},{3,195},{32,35},{33,32},{34,33},{35,34},{6... | collective-permute-start | bytes 958472 | tf_op jit(solution)/shard_map/ppermute | solution.py:561
  36.9 9.7 %collective-permute-start.7 = (bf16[2,48,1664]{2,1,0:T(8,128)(2,1)S(1)}, bf16[2,48,1664]{2,1,0:T(8,128)(2,1)S(1)}, u32[]{:S(2)}, u32[]{:S(2)}) collective-permute-start(bf16[2,48,1664]{2,1,0:T(8,128)(2,1)S(1)} %shard_map.167.refs_0_), channel_id=1, source_target_pairs={{0,192},{1,193},{2,194},{3,195},{32,35},{33,32},{34,33},{35,34},{6... | collective-permute-start | bytes 958472 | tf_op jit(solution)/shard_map/ppermute | solution.py:561
  37.2 9.5 %collective-permute-start.6 = (bf16[2,48,1664]{2,1,0:T(8,128)(2,1)S(1)}, bf16[2,48,1664]{2,1,0:T(8,128)(2,1)S(1)}, u32[]{:S(2)}, u32[]{:S(2)}) collective-permute-start(bf16[2,48,1664]{2,1,0:T(8,128)(2,1)S(1)} %shard_map.168.refs_1_), channel_id=1, source_target_pairs={{0,64},{1,65},{2,66},{3,67},{32,33},{33,34},{34,35},{35,32},{64,12... | collective-permute-start | bytes 958472 | tf_op jit(solution)/shard_map/ppermute | solution.py:561
  42.7 9.2 %collective-permute-start.10 = (bf16[2,48,1664]{2,1,0:T(8,128)(2,1)S(1)}, bf16[2,48,1664]{2,1,0:T(8,128)(2,1)S(1)}, u32[]{:S(2)}, u32[]{:S(2)}) collective-permute-start(bf16[2,48,1664]{2,1,0:T(8,128)(2,1)S(1)} %shard_map.167.refs_0_), channel_id=1, source_target_pairs={{0,32},{32,0},{64,96},{96,64},{128,160},{160,128},{192,224},{224,1... | collective-permute-start | bytes 958472 | tf_op jit(solution)/shard_map/ppermute | solution.py:564
  46.1 7.8 %collective-permute-start.11 = (bf16[2,48,1664]{2,1,0:T(8,128)(2,1)S(1)}, bf16[2,48,1664]{2,1,0:T(8,128)(2,1)S(1)}, u32[]{:S(2)}, u32[]{:S(2)}) collective-permute-start(bf16[2,48,1664]{2,1,0:T(8,128)(2,1)S(1)} %shard_map.168.refs_1_), channel_id=1, source_target_pairs={{0,32},{32,0},{64,96},{96,64},{128,160},{160,128},{192,224},{224,1... | collective-permute-start | bytes 958472 | tf_op jit(solution)/shard_map/ppermute | solution.py:564
  46.3 7.8 %collective-permute-start.12 = (bf16[2,48,1664]{2,1,0:T(8,128)(2,1)S(1)}, bf16[2,48,1664]{2,1,0:T(8,128)(2,1)S(1)}, u32[]{:S(2)}, u32[]{:S(2)}) collective-permute-start(bf16[2,48,1664]{2,1,0:T(8,128)(2,1)S(1)} %collective-permute-done.4.refs_2_), channel_id=1, source_target_pairs={{0,32},{32,0},{64,96},{96,64},{128,160},{160,128},{192,224},{224,1... | collective-permute-start | bytes 958472 | tf_op jit(solution)/shard_map/ppermute | solution.py:564
  46.7 7.8 %collective-permute-start.8 = (bf16[2,48,1664]{2,1,0:T(8,128)(2,1)S(1)}, bf16[2,48,1664]{2,1,0:T(8,128)(2,1)S(1)}, u32[]{:S(2)}, u32[]{:S(2)}) collective-permute-start(bf16[2,48,1664]{2,1,0:T(8,128)(2,1)S(1)} %collective-permute-done.4.refs_2_), channel_id=1, source_target_pairs={{0,64},{1,65},{2,66},{3,67},{32,33},{33,34},{34,35},{35,32},{64,12... | collective-permute-start | bytes 958472 | tf_op jit(solution)/shard_map/ppermute | solution.py:561
  46.7 9.6 %collective-permute-start.9 = (bf16[2,48,1664]{2,1,0:T(8,128)(2,1)S(1)}, bf16[2,48,1664]{2,1,0:T(8,128)(2,1)S(1)}, u32[]{:S(2)}, u32[]{:S(2)}) collective-permute-start(bf16[2,48,1664]{2,1,0:T(8,128)(2,1)S(1)} %collective-permute-done.5.refs_7_), channel_id=1, source_target_pairs={{0,192},{1,193},{2,194},{3,195},{32,35},{33,32},{34,33},{35,34},{6... | collective-permute-start | bytes 958472 | tf_op jit(solution)/shard_map/ppermute | solution.py:561
  51.9 4.4 %collective-permute-start.17 = (bf16[2,48,1664]{2,1,0:T(8,128)(2,1)S(1)}, bf16[2,48,1664]{2,1,0:T(8,128)(2,1)S(1)}, u32[]{:S(2)}, u32[]{:S(2)}) collective-permute-start(bf16[2,48,1664]{2,1,0:T(8,128)(2,1)S(1)} %collective-permute-done.5.refs_7_), channel_id=1, source_target_pairs={{0,32},{32,0},{64,96},{96,64},{128,160},{160,128},{192,224},{224,1... | collective-permute-start | bytes 958472 | tf_op jit(solution)/shard_map/ppermute | solution.py:564
  54.0 2.4 %collective-permute-start.13 = (bf16[2,48,1664]{2,1,0:T(8,128)(2,1)S(1)}, bf16[2,48,1664]{2,1,0:T(8,128)(2,1)S(1)}, u32[]{:S(2)}, u32[]{:S(2)}) collective-permute-start(bf16[2,48,1664]{2,1,0:T(8,128)(2,1)S(1)} %collective-permute-done.6.refs_3_), channel_id=1, source_target_pairs={{0,32},{32,0},{64,96},{96,64},{128,160},{160,128},{192,224},{224,1... | collective-permute-start | bytes 958472 | tf_op jit(solution)/shard_map/ppermute | solution.py:564
  54.1 2.3 %collective-permute-start.16 = (bf16[2,48,1664]{2,1,0:T(8,128)(2,1)S(1)}, bf16[2,48,1664]{2,1,0:T(8,128)(2,1)S(1)}, u32[]{:S(2)}, u32[]{:S(2)}) collective-permute-start(bf16[2,48,1664]{2,1,0:T(8,128)(2,1)S(1)} %collective-permute-done.7.refs_6_), channel_id=1, source_target_pairs={{0,32},{32,0},{64,96},{96,64},{128,160},{160,128},{192,224},{224,1... | collective-permute-start | bytes 958472 | tf_op jit(solution)/shard_map/ppermute | solution.py:564
  54.5 3.1 %collective-permute-start.14 = (bf16[2,48,1664]{2,1,0:T(8,128)(2,1)S(1)}, bf16[2,48,1664]{2,1,0:T(8,128)(2,1)S(1)}, u32[]{:S(2)}, u32[]{:S(2)}) collective-permute-start(bf16[2,48,1664]{2,1,0:T(8,128)(2,1)S(1)} %collective-permute-done.8.refs_4_), channel_id=1, source_target_pairs={{0,32},{32,0},{64,96},{96,64},{128,160},{160,128},{192,224},{224,1... | collective-permute-start | bytes 958472 | tf_op jit(solution)/shard_map/ppermute | solution.py:564
  56.3 1.7 %collective-permute-start.15 = (bf16[2,48,1664]{2,1,0:T(8,128)(2,1)S(1)}, bf16[2,48,1664]{2,1,0:T(8,128)(2,1)S(1)}, u32[]{:S(2)}, u32[]{:S(2)}) collective-permute-start(bf16[2,48,1664]{2,1,0:T(8,128)(2,1)S(1)} %collective-permute-done.9.refs_5_), channel_id=1, source_target_pairs={{0,32},{32,0},{64,96},{96,64},{128,160},{160,128},{192,224},{224,1... | collective-permute-start | bytes 958472 | tf_op jit(solution)/shard_map/ppermute | solution.py:564
  63.4 5.0 %collective-permute-start.19 = (bf16[4,48,1664]{2,1,0:T(8,128)(2,1)S(1)}, bf16[4,48,1664]{2,1,0:T(8,128)(2,1)S(1)}, u32[]{:S(2)}, u32[]{:S(2)}) collective-permute-start(bf16[4,48,1664]{2,1,0:T(8,128)(2,1)S(1)} %get-tuple-element.83), channel_id=1, source_target_pairs={{0,32},{32,0},{64,96},{96,64},{128,160},{160,128},{192,224},{224,1... | collective-permute-start | bytes 1916936 | tf_op jit(solution)/shard_map/ppermute | solution.py:564
  65.0 4.4 %collective-permute-start.21 = (bf16[4,48,1664]{2,1,0:T(8,128)(2,1)S(1)}, bf16[4,48,1664]{2,1,0:T(8,128)(2,1)S(1)}, u32[]{:S(2)}, u32[]{:S(2)}) collective-permute-start(bf16[4,48,1664]{2,1,0:T(8,128)(2,1)S(1)} %get-tuple-element.86), channel_id=1, source_target_pairs={{0,32},{32,0},{64,96},{96,64},{128,160},{160,128},{192,224},{224,1... | collective-permute-start | bytes 1916936 | tf_op jit(solution)/shard_map/ppermute | solution.py:564
  66.4 5.3 %collective-permute-start.23 = (bf16[4,48,1664]{2,1,0:T(8,128)(2,1)S(1)}, bf16[4,48,1664]{2,1,0:T(8,128)(2,1)S(1)}, u32[]{:S(2)}, u32[]{:S(2)}) collective-permute-start(bf16[4,48,1664]{2,1,0:T(8,128)(2,1)S(1)} %get-tuple-element.89), channel_id=1, source_target_pairs={{0,32},{32,0},{64,96},{96,64},{128,160},{160,128},{192,224},{224,1... | collective-permute-start | bytes 1916936 | tf_op jit(solution)/shard_map/ppermute | solution.py:564
  68.0 4.9 %collective-permute-start.18 = (bf16[4,48,1664]{2,1,0:T(8,128)(2,1)S(1)}, bf16[4,48,1664]{2,1,0:T(8,128)(2,1)S(1)}, u32[]{:S(2)}, u32[]{:S(2)}) collective-permute-start(bf16[4,48,1664]{2,1,0:T(8,128)(2,1)S(1)} %get-tuple-element.80), channel_id=1, source_target_pairs={{0,32},{32,0},{64,96},{96,64},{128,160},{160,128},{192,224},{224,1... | collective-permute-start | bytes 1916936 | tf_op jit(solution)/shard_map/ppermute | solution.py:564
  68.7 9.6 %collective-permute-start.20 = (bf16[4,48,1664]{2,1,0:T(8,128)(2,1)S(1)}, bf16[4,48,1664]{2,1,0:T(8,128)(2,1)S(1)}, u32[]{:S(2)}, u32[]{:S(2)}) collective-permute-start(bf16[4,48,1664]{2,1,0:T(8,128)(2,1)S(1)} %shard_map.174), channel_id=1, source_target_pairs={{0,192},{1,193},{2,194},{3,195},{32,35},{33,32},{34,33},{35,34},{6... | collective-permute-start | bytes 1916936 | tf_op jit(solution)/shard_map/ppermute | solution.py:561
  69.4 29.7 %copy-start.1 = (bf16[1,128,1536]{2,1,0:T(8,128)(2,1)S(1)}, bf16[1,128,1536]{2,1,0:T(8,128)(2,1)}, u32[]{:S(2)}) copy-start(bf16[1,128,1536]{2,1,0:T(8,128)(2,1)} %up_map.3) | copy-start | bytes 1179652
  69.7 11.2 %collective-permute-start.22 = (bf16[4,48,1664]{2,1,0:T(8,128)(2,1)S(1)}, bf16[4,48,1664]{2,1,0:T(8,128)(2,1)S(1)}, u32[]{:S(2)}, u32[]{:S(2)}) collective-permute-start(bf16[4,48,1664]{2,1,0:T(8,128)(2,1)S(1)} %shard_map.176), channel_id=1, source_target_pairs={{0,128},{1,129},{2,130},{3,131},{32,34},{33,35},{34,32},{35,33},{6... | collective-permute-start | bytes 1916936 | tf_op jit(solution)/shard_map/ppermute | solution.py:561
  72.0 15.7 %collective-permute-start.24 = (bf16[4,48,1664]{2,1,0:T(8,128)(2,1)S(1)}, bf16[4,48,1664]{2,1,0:T(8,128)(2,1)S(1)}, u32[]{:S(2)}, u32[]{:S(2)}) collective-permute-start(bf16[4,48,1664]{2,1,0:T(8,128)(2,1)S(1)} %shard_map.178), channel_id=1, source_target_pairs={{0,64},{1,65},{2,66},{3,67},{32,33},{33,34},{34,35},{35,32},{64,12... | collective-permute-start | bytes 1916936 | tf_op jit(solution)/shard_map/ppermute | solution.py:561
  88.4 7.0 %collective-permute-start.25 = (bf16[48,2048]{1,0:T(8,128)(2,1)S(1)}, bf16[48,2048]{1,0:T(8,128)(2,1)S(1)}, u32[]{:S(2)}, u32[]{:S(2)}) collective-permute-start(bf16[48,2048]{1,0:T(8,128)(2,1)S(1)} %get-tuple-element.91), channel_id=1, source_target_pairs={{0,3},{1,0},{2,1},{3,2},{32,224},{33,225},{34,226},{35,227},{64,67... | collective-permute-start | bytes 589832 | tf_op jit(solution)/shard_map/ppermute | solution.py:561
  90.7 6.1 %collective-permute-start.26 = (bf16[48,2048]{1,0:T(8,128)(2,1)S(1)}, bf16[48,2048]{1,0:T(8,128)(2,1)S(1)}, u32[]{:S(2)}, u32[]{:S(2)}) collective-permute-start(bf16[48,2048]{1,0:T(8,128)(2,1)S(1)} %get-tuple-element.92), channel_id=1, source_target_pairs={{0,2},{1,3},{2,0},{3,1},{32,160},{33,161},{34,162},{35,163},{64,66... | collective-permute-start | bytes 589832 | tf_op jit(solution)/shard_map/ppermute | solution.py:561
  91.0 8.1 %collective-permute-start.27 = (bf16[48,2048]{1,0:T(8,128)(2,1)S(1)}, bf16[48,2048]{1,0:T(8,128)(2,1)S(1)}, u32[]{:S(2)}, u32[]{:S(2)}) collective-permute-start(bf16[48,2048]{1,0:T(8,128)(2,1)S(1)} %get-tuple-element.93), channel_id=1, source_target_pairs={{0,1},{1,2},{2,3},{3,0},{32,96},{33,97},{34,98},{35,99},{64,65},{6... | collective-permute-start | bytes 589832 | tf_op jit(solution)/shard_map/ppermute | solution.py:561
  100.3 3.8 %collective-permute-start.28 = (bf16[24,1536]{1,0:T(8,128)(2,1)S(1)}, bf16[24,1536]{1,0:T(8,128)(2,1)S(1)}, u32[]{:S(2)}, u32[]{:S(2)}) collective-permute-start(bf16[24,1536]{1,0:T(8,128)(2,1)S(1)} %get-tuple-element.96), channel_id=1, source_target_pairs={{0,32},{32,0},{64,96},{96,64},{128,160},{160,128},{192,224},{224,1... | collective-permute-start | bytes 221192 | tf_op jit(solution)/shard_map/ppermute | solution.py:564
  105.1 12.0 %all-to-all-start.1 = ((bf16[8,8,1152]{2,1,0:T(8,128)(2,1)}), bf16[8,8,1152]{2,1,0:T(8,128)(2,1)S(1)}, u32[]{:S(2)}, u32[]{:S(2)}) async-start(bf16[8,8,1152]{2,1,0:T(8,128)(2,1)} %bitcast.7), calls=%async_computation.1 | async-start | bytes 294912 | tf_op jit(solution)/shard_map/all_to_all | solution.py:694
  (5 other events, 110.7 us)
